TPU v7x, 512 devices: a whole 4x4x16 slice. The times are simulated.
512 devices in a mesh: seq: 64 (over y_lo, z, core), clip: 8 (over x, y_hi).
Axes of the slice: x: 4, y: 4 (y_hi: 2, y_lo: 2; y = y_hi * 2 + y_lo), z: 16, core: 2. Of those that a mesh axis runs over, the one named last changes fastest.
Arguments:
- block_input: bfloat16 [8, 64, 128, 1152], P('clip', 'seq'), may hold values from -8 to 8
- out_grad: bfloat16 [8, 64, 128, 1152], P('clip', 'seq'), may hold values from -16 to 16
- spatial_qkv: bfloat16 [8, 64, 128, 3456], P('clip', 'seq'), may hold values from -32 to 32, as said below
- norm_gain: float32 [1152], replicated, may hold values from 0.25 to 1.75
- qkv_weight: bfloat16 [1152, 3456], P('seq'), may hold values from -1 to 1
- qkv_bias: float32 [3456], replicated, may hold values from -3 to 3
- out_weight: bfloat16 [1152, 1152], P('seq'), may hold values from -0.1875 to 0.1875
- spatial_out_weight: bfloat16 [1152, 1152], P('seq'), may hold values from -0.1875 to 0.1875
- grad_sums: float32 [9, 1152], P(None, 'seq'), may hold values from -6 to 6
Outputs:
- resid_grad: bfloat16 [8, 64, 128, 1152], P('clip', 'seq')
- spatial_qkv_grad: bfloat16 [8, 64, 128, 3456], P('clip', 'seq')
- grad_totals: float32 [9, 1152], P(None, 'seq')
Inputs may be any that keep to these rules, and one draw needn't show every extreme that they name: `spatial_qkv`: the last dimension holds queries, keys and values in this order, each as 16 heads of 72 entries.
All inputs are finite; a program needn't handle non-finite values.
Results may differ from a plain program's by a relative error of at most 0.012.
The roundings to bfloat16 on the way count: a program that leaves them out, or rounds other values in their place, can miss the bound.
Values may be sent and summed in bfloat16 or wider, within the bound.
A program may use at most 128 MiB of HBM per device.

v0:
```python
import math

import jax
import jax.numpy as jnp
from jax import lax
from jax.sharding import PartitionSpec as P

HEADS = 16


EPS = 1e-06


def side_by_side(arrays, axis, dim, along):
    ends, at = ([], 0)
    for a in arrays[:-1]:
        at += a.shape[along]
        ends.append(at)
    both = jnp.concatenate(arrays, axis=along)
    return tuple(jnp.split(lax.all_gather(both, axis, axis=dim, tiled=True), ends, axis=along))


def in_one_piece(arrays, axis, split_dim, concat_dim, along):
    ends, at = ([], 0)
    for a in arrays[:-1]:
        at += a.shape[along]
        ends.append(at)
    both = jnp.concatenate(arrays, axis=along)
    return tuple(
        jnp.split(
            lax.all_to_all(both, axis, split_axis=split_dim, concat_axis=concat_dim, tiled=True),
            ends,
            axis=along,
        )
    )


def split_up(x, dim, length):
    lengths = x.shape
    blocks = x.reshape(*lengths[:dim], length, lengths[dim] // length, *lengths[dim + 1 :])
    return jnp.moveaxis(blocks, dim, 0)


def sum_at_owner(x, axis, dim):
    length = lax.axis_size(axis)
    blocks = lax.all_to_all(split_up(x, dim, length), axis, 0, 0, tiled=True)
    return jnp.sum(blocks, axis=0)


def from_everyone(x, axis):
    copies = jnp.broadcast_to(x, (lax.axis_size(axis), *x.shape))
    return lax.all_to_all(copies, axis, split_axis=0, concat_axis=0, tiled=True)


def taken_together(x, axis):
    everything = from_everyone(x, axis)
    return jnp.sum(everything, axis=0)


def attention_back(queries, key_side, value_side, grad_out, layout, factor):
    key_layout = layout.replace("l", "m")
    scores = (
        jnp.einsum(
            layout + "," + key_layout + "->bhlm",
            queries,
            key_side,
            preferred_element_type=jnp.float32,
        )
        * factor
    )
    weights = jax.nn.softmax(scores, axis=-1)
    weights_half = weights.astype(jnp.bfloat16)
    grad_value = jnp.einsum(
        "bhlm," + layout + "->" + key_layout,
        weights_half,
        grad_out,
        preferred_element_type=jnp.float32,
    ).astype(jnp.bfloat16)
    grad_weight = jnp.einsum(
        layout + "," + key_layout + "->bhlm",
        grad_out,
        value_side,
        preferred_element_type=jnp.float32,
    )
    grad_score = (
        weights * (grad_weight - jnp.sum(weights * grad_weight, axis=-1, keepdims=True)) * factor
    ).astype(jnp.bfloat16)
    grad_query = jnp.einsum(
        "bhlm," + key_layout + "->" + layout,
        grad_score,
        key_side,
        preferred_element_type=jnp.float32,
    ).astype(jnp.bfloat16)
    grad_key = jnp.einsum(
        "bhlm," + layout + "->" + key_layout,
        grad_score,
        queries,
        preferred_element_type=jnp.float32,
    ).astype(jnp.bfloat16)
    return (grad_query, grad_key, grad_value)


def per_device(
    block_input,
    out_grad,
    spatial_qkv,
    norm_gain,
    qkv_weight,
    qkv_bias,
    out_weight,
    spatial_out_weight,
    grad_sums,
):
    features = block_input.shape[3]
    head_dim = features // HEADS
    factor = 1.0 / math.sqrt(head_dim)
    full_qkv, full_out, full_spatial = side_by_side(
        (qkv_weight, out_weight, spatial_out_weight), "seq", 0, 1
    )
    patch_input, patch_grad = in_one_piece((block_input, out_grad), "seq", 2, 1, 0)
    frames, patches = (patch_input.shape[1], patch_input.shape[2])
    rows_in = patch_input.reshape(frames * patches, features).astype(jnp.float32)
    centred = rows_in - jnp.mean(rows_in, axis=-1, keepdims=True)
    inv_std = lax.rsqrt(jnp.mean(centred * centred, axis=-1, keepdims=True) + EPS)
    normal_rows = centred * inv_std
    normed = (normal_rows * norm_gain).astype(jnp.bfloat16)
    qkv_rows = (jnp.dot(normed, full_qkv, preferred_element_type=jnp.float32) + qkv_bias).astype(
        jnp.bfloat16
    )
    qkv_heads = qkv_rows.reshape(frames, patches, 3, HEADS, head_dim)
    grad_attn = jnp.einsum(
        "td,ed->te",
        patch_grad.reshape(frames * patches, features),
        full_out,
        preferred_element_type=jnp.float32,
    ).astype(jnp.bfloat16)
    grad_query, grad_key, grad_value = attention_back(
        qkv_heads[:, :, 0],
        qkv_heads[:, :, 1],
        qkv_heads[:, :, 2],
        grad_attn.reshape(frames, patches, HEADS, head_dim),
        "lbhe",
        factor,
    )
    grad_qkv = jnp.stack([grad_query, grad_key, grad_value], axis=2).reshape(
        frames * patches, 3 * features
    )
    grad_normed = jnp.einsum("tc,dc->td", grad_qkv, full_qkv, preferred_element_type=jnp.float32)
    grad_hat = grad_normed * norm_gain
    branch = inv_std * (
        grad_hat
        - jnp.mean(grad_hat, axis=-1, keepdims=True)
        - normal_rows * jnp.mean(grad_hat * normal_rows, axis=-1, keepdims=True)
    )
    branch_half = branch.astype(jnp.bfloat16).reshape(1, frames, patches, features)
    frame_branch = lax.all_to_all(branch_half, "seq", split_axis=1, concat_axis=2, tiled=True)
    resid_grad = (out_grad.astype(jnp.float32) + frame_branch.astype(jnp.float32)).astype(
        jnp.bfloat16
    )
    local_frames, local_patches = (resid_grad.shape[1], resid_grad.shape[2])
    resid_rows = resid_grad.reshape(local_frames * local_patches, features)
    grad_sattn = jnp.einsum(
        "td,ed->te", resid_rows, full_spatial, preferred_element_type=jnp.float32
    ).astype(jnp.bfloat16)
    spatial_heads = spatial_qkv.reshape(local_frames, local_patches, 3, HEADS, head_dim)
    spatial_query, spatial_key, spatial_value = attention_back(
        spatial_heads[:, :, 0],
        spatial_heads[:, :, 1],
        spatial_heads[:, :, 2],
        grad_sattn.reshape(local_frames, local_patches, HEADS, head_dim),
        "blhe",
        factor,
    )
    spatial_grad = jnp.stack([spatial_query, spatial_key, spatial_value], axis=2).reshape(
        local_frames * local_patches, 3 * features
    )
    partial_value = jnp.concatenate(
        [
            jnp.sum(grad_normed * normal_rows, axis=0)[None],
            jnp.sum(grad_qkv.astype(jnp.float32), axis=0).reshape(3, features),
            jnp.sum(out_grad.astype(jnp.float32).reshape(-1, features), axis=0)[None],
            jnp.sum(spatial_grad.astype(jnp.float32), axis=0).reshape(3, features),
            jnp.sum(resid_rows.astype(jnp.float32), axis=0)[None],
        ],
        axis=0,
    )
    total_tokens = (
        block_input.shape[0]
        * lax.axis_size("clip")
        * local_frames
        * lax.axis_size("seq")
        * local_patches
    )
    grad_scale = 1.0 / math.sqrt(total_tokens)
    seq_share = sum_at_owner(partial_value, "seq", 1)
    share_part = taken_together(seq_share, "clip")
    grad_totals = grad_sums + share_part * grad_scale
    return (
        resid_grad,
        spatial_grad.reshape(1, local_frames, local_patches, 3 * features),
        grad_totals,
    )


def solution(mesh):
    in_specs = (
        P("clip", "seq", None, None),
        P("clip", "seq", None, None),
        P("clip", "seq", None, None),
        P(),
        P("seq", None),
        P(),
        P("seq", None),
        P("seq", None),
        P(None, "seq"),
    )
    out_specs = (P("clip", "seq", None, None), P("clip", "seq", None, None), P(None, "seq"))
    return jax.shard_map(
        per_device, mesh=mesh, in_specs=in_specs, out_specs=out_specs, check_vma=False
    )
```

profile of v0, /device:TPU:1, one launch (start us, length us, event | category | flops | bytes accessed | tf_op | source)
XLA Modules:
  0.0 311.7 jit_solution(8581119019559039677)
XLA Ops:
  7.2 1.7 maximum_bitcast_fusion
  9.0 1.4 copy.128
  10.4 1.4 copy.129
  11.8 1.3 pad_maximum_fusion.2
  13.1 57.9 %all_to_all.28 = bf16[2,1,128,1152]{3,0,1,2:T(2,128)(2,1)S(1)} all-to-all(bf16[2,1,128,1152]{3,0,1,2:T(2,128)(2,1)S(1)} %pad_maximum_fusion.2), channel_id=1, replica_groups=mesh['seq'=64,'clip'=8] {'seq'}, dimensions={2} | all-to-all | bytes 1179648 | tf_op jit(solution)/shard_map/all_to_all | solution.py:31
  71.0 0.8 fusion.96
  72.0 0.2 fusion.54
  72.2 104.4 %all-gather.3.cloned.1.call-done = bf16[64,18,5760]{2,1,0:T(8,128)(2,1)} async-done(((bf16[1,18,5760]{2,1,0:T(8,128)(2,1)}), bf16[64,18,5760]{2,1,0:T(8,128)(2,1)}) %all-gather.3.cloned.1.call-update) | async-done | bytes 13271056 | tf_op jit(solution)/shard_map/all_gather | solution.py:20
  176.6 17.8 %reshape.241 = bf16[1152,5760]{1,0:T(8,128)(2,1)} reshape(bf16[64,18,5760]{2,1,0:T(8,128)(2,1)} %all-gather.3.cloned.1.call-done) | data formatting | bytes 26542080
  194.5 2.7 fusion.18
  197.2 0.9 reshape.229
  198.2 4.7 %fusion.11 = bf16[128,3456]{1,0:T(8,128)(2,1)S(1)} fusion(bf16[1152,5760]{1,0:T(8,128)(2,1)} %reshape.241, f32[3456]{0:T(1024)S(1)} %copy-done.5, bf16[1,1,128,1152]{3,2,1,0:T(8,128)(2,1)S(1)} %get-tuple-element.34, f32[1152]{0:T(1024)S(1)} %copy-done.3, f32[128]{0:T(128)S(1)} %broadcast_multiply_fusion.2, f32[128]{0:T(128)S(1)} %add_rsqrt_fusion), kind=kOutput, calls=%fused_computation.9 | convolution fusion | flops 1020837888 | bytes 9161728 | tf_op jit(solution)/shard_map/dot_general | solution.py:127
  202.9 2.8 reshape.227
  205.7 0.3 fusion.95
  205.9 0.4 fusion.67
  206.4 1.6 fusion.97
  208.0 1.6 fusion.38
  209.6 2.1 fusion.37
  211.7 2.1 fusion.36
  213.9 0.6 convert_reduce_fusion
  214.4 1.0 copy.138
  215.5 1.8 reshape.230
  217.3 5.9 %fusion.66 = (f32[1152]{0:T(1024)S(1)}, f32[128]{0:T(128)S(1)}, f32[128]{0:T(128)S(1)}, f32[128,1152]{1,0:T(8,128)S(1)}) fusion(bf16[1,1,128,1152]{3,2,1,0:T(8,128)(2,1)S(1)} %get-tuple-element.34, f32[128]{0:T(128)S(1)} %broadcast_multiply_fusion.2, f32[128]{0:T(128)S(1)} %add_rsqrt_fusion, f32[1152]{0:T(1024)S(1)} %copy-done.3, ...), kind=kOutput, calls=%fused_computation.69 | convolution fusion | flops 1020541568 | bytes 9743360 | tf_op jit(solution)/shard_map/tc,dc->td/dot_general | solution.py:148
  223.2 0.3 fusion.65
  223.6 0.8 reshape.231
  224.4 8.6 %all-to-all-start.1 = ((bf16[1,64,2,1152]{3,2,0,1:T(2,128)(2,1)}), bf16[1,64,2,1152]{3,2,0,1:T(2,128)(2,1)S(1)}, u32[]{:S(2)}, u32[]{:S(2)}) async-start(bf16[1,64,2,1152]{3,2,0,1:T(2,128)(2,1)} %bitcast.12), calls=%async_computation.1 | async-start | bytes 589824 | tf_op jit(solution)/shard_map/all_to_all | solution.py:156
  233.2 1.0 copy.140
  234.2 1.5 fusion.98
  236.0 20.4 %all-to-all-done.1 = bf16[1,64,2,1152]{3,2,0,1:T(2,128)(2,1)S(1)} async-done(((bf16[1,64,2,1152]{3,2,0,1:T(2,128)(2,1)}), bf16[1,64,2,1152]{3,2,0,1:T(2,128)(2,1)S(1)}, u32[]{:S(2)}, u32[]{:S(2)}) %all-to-all-start.1) | async-done | bytes 294944 | tf_op jit(solution)/shard_map/all_to_all | solution.py:156
  256.6 2.8 fusion.21
  259.3 0.2 copy.141
  259.5 0.4 fusion.77
  259.9 1.7 fusion.41
  261.6 2.8 fusion.39
  264.4 2.8 fusion.40
  267.3 1.5 convert_reduce_fusion.1
  269.0 0.2 copy.145
  269.2 0.3 reshape.242
  269.5 18.7 %all_to_all.29 = f32[64,1,162]{2,1,0:T(1,128)S(1)} all-to-all(f32[64,1,162]{2,1,0:T(1,128)S(1)} %reshape.242), channel_id=1, replica_groups=mesh['seq'=64,'clip'=8] {'seq'}, dimensions={0} | all-to-all | bytes 82944 | tf_op jit(solution)/shard_map/all_to_all | solution.py:46
  288.2 0.6 broadcast.99
  288.7 0.8 reduce.13
  289.6 0.2 reshape.243
  289.9 0.7 reshape.244
  290.6 6.3 %all-to-all-start.3 = ((f32[8,1,162]{2,1,0:T(1,128)}), f32[8,1,162]{2,1,0:T(1,128)S(1)}, u32[]{:S(2)}, u32[]{:S(2)}) async-start(f32[8,1,162]{2,1,0:T(1,128)} %reshape.244), calls=%async_computation.3 | async-start | bytes 16384 | tf_op jit(solution)/shard_map/all_to_all | solution.py:52
  296.9 1.6 copy.147
  298.6 4.9 %all-to-all-done.3 = f32[8,1,162]{2,1,0:T(1,128)S(1)} async-done(((f32[8,1,162]{2,1,0:T(1,128)}), f32[8,1,162]{2,1,0:T(1,128)S(1)}, u32[]{:S(2)}, u32[]{:S(2)}) %all-to-all-start.3) | async-done | bytes 5216 | tf_op jit(solution)/shard_map/all_to_all | solution.py:52
  303.5 0.7 reduce.14
  304.3 0.6 multiply_add_fusion
  (35 shorter events, 1.2 us)
Async XLA Ops:
  7.2 169.5 %all-gather.3.cloned.1.call-start = ((), (), s32[]{:S(2)}) async-start(), calls=%async_computation.4 | async-start | bytes 17971200 | tf_op jit(solution)/shard_map/all_gather | solution.py:20
  194.5 3.7 %copy-start.3 = (f32[1152]{0:T(1024)S(1)}, f32[1152]{0:T(1024)}, u32[]{:S(2)}) copy-start(f32[1152]{0:T(1024)} %param.12) | copy-start | bytes 13828
  194.5 3.7 %copy-start.5 = (f32[3456]{0:T(1024)S(1)}, f32[3456]{0:T(1024)}, u32[]{:S(2)}) copy-start(f32[3456]{0:T(1024)} %param.14) | copy-start | bytes 41476
  217.3 15.7 %copy-start = (bf16[1,1,128,1152]{3,2,1,0:T(8,128)(2,1)S(1)}, bf16[1,1,128,1152]{3,2,1,0:T(8,128)(2,1)}, u32[]{:S(2)}) copy-start(bf16[1,1,128,1152]{3,2,1,0:T(8,128)(2,1)} %param.10) | copy-start | bytes 884740
  223.2 10.0 %copy-start.1 = (bf16[1,1,128,3456]{3,2,1,0:T(8,128)(2,1)S(1)}, bf16[1,1,128,3456]{3,2,1,0:T(8,128)(2,1)}, u32[]{:S(2)}) copy-start(bf16[1,1,128,3456]{3,2,1,0:T(8,128)(2,1)} %param.11) | copy-start | bytes 2654212
  224.4 32.0 %all-to-all-start.1 = ((bf16[1,64,2,1152]{3,2,0,1:T(2,128)(2,1)}), bf16[1,64,2,1152]{3,2,0,1:T(2,128)(2,1)S(1)}, u32[]{:S(2)}, u32[]{:S(2)}) async-start(bf16[1,64,2,1152]{3,2,0,1:T(2,128)(2,1)} %bitcast.12), calls=%async_computation.1 | async-start | bytes 589824 | tf_op jit(solution)/shard_map/all_to_all | solution.py:156
  256.5 3.0 copy-start.2
  268.9 35.4 %copy-start.4 = (f32[9,18]{1,0:T(8,128)S(1)}, f32[9,18]{1,0:T(8,128)}, u32[]{:S(2)}) copy-start(f32[9,18]{1,0:T(8,128)} %param.17) | copy-start | bytes 1948
  290.6 12.8 %all-to-all-start.3 = ((f32[8,1,162]{2,1,0:T(1,128)}), f32[8,1,162]{2,1,0:T(1,128)S(1)}, u32[]{:S(2)}, u32[]{:S(2)}) async-start(f32[8,1,162]{2,1,0:T(1,128)} %reshape.244), calls=%async_computation.3 | async-start | bytes 16384 | tf_op jit(solution)/shard_map/all_to_all | solution.py:52
Sparse Core Ops, SparseCore 0:
  10.7 165.8 all-gather.2
where the time goes:
time: 313 us; the launch traced here: 312 us
  waiting for transfers between devices  130 us (42%)
  blocking collectives  76.6 us (24%)
  local copies, waits for them, and re-layouts  34.8 us (11%)
  matrix products  33.1 us (11%)
  starting transfers between devices  15 us (5%)
  between operations  14.4 us (5%)
  other arithmetic  8.26 us (3%)
    all_gather x1, waiting for transfers between devices, side_by_side(): lax.all_gather(both, axis, axis=dim, tiled=True)  104 us
    all_to_all x1, blocking collectives, in_one_piece(): lax.all_to_all(both, axis, split_axis=split_dim, concat_axis=concat_dim,...  57.9 us
    unnamed x25, local copies, waits for them, and re-layouts  24.6 us
    all_to_all x1, waiting for transfers between devices, per_device(): lax.all_to_all(branch_half, 'seq', split_axis=1, concat_axis=2, tiled=True)  20.4 us
    all_to_all x1, blocking collectives, sum_at_owner(): blocks = lax.all_to_all(split_up(x, dim, length), axis, 0, 0, tiled=True)  18.7 us
    all_to_all x1, starting transfers between devices, per_device(): lax.all_to_all(branch_half, 'seq', split_axis=1, concat_axis=2, tiled=True)  8.6 us
    all_to_all x1, starting transfers between devices, from_everyone(): return lax.all_to_all(copies, axis, split_axis=0, concat_axis=0, tiled=True)  6.31 us
  transfers between devices with their start and end apart: 3, of which 3 were waited for; matrix products, arithmetic and copies ran while one was open for 3% of the time, Pallas kernels for 0%

commit v1 on v0

v1 whole, which is shorter than its diff:
```python
import functools
import math

import jax
import jax.numpy as jnp
from jax import lax
from jax.experimental import pallas as pl
from jax.experimental.pallas import tpu as pltpu
from jax.sharding import PartitionSpec as P

HEADS = 16
EPS = 1e-06
MESH = pl.DeviceIdType.MESH
F32 = jnp.float32
BF16 = jnp.bfloat16

D = 1152
CH = 384
NCH = 16
NZ = 16
UNIT = 144
HALF = ((0, 80), (80, 64))


def dev(x, y, z, c):
    return {"clip": x * 2 + y // 2, "seq": (y % 2) * 32 + z * 2 + c}


def place():
    s, q = lax.axis_index("seq"), lax.axis_index("clip")
    x = q // 2
    y = (q % 2) * 2 + s // 32
    z = (s // 2) % 16
    c = s % 2
    return x, y, z, c


def gather_kernel(
    ws, xg, w_out, r_out, zbuf, wbuf, own, loc, swap_s, swap_r, zsend, zrecv, a_send, a_recv,
    p_send, p_recv, d_send, d_recv, h_sem,
):
    x, y, z, c = place()
    s, q = lax.axis_index("seq"), lax.axis_index("clip")
    ylo = s // 32
    sib = dev(x, y, z, 1 - c)

    def near(axis, step):
        if axis == 0:
            return (x + step + 4) % 4, y
        return x, (y + step + 4) % 4

    barrier = pltpu.get_barrier_semaphore()
    partners = [
        sib,
        dev(x, y, (z + 1) % NZ, c),
        dev(x, y, (z + NZ - 1) % NZ, c),
        dev(x, y, (z + 2) % NZ, c),
        dev(x, y, (z + NZ - 2) % NZ, c),
        dev(*near(0, 1), z, c),
        dev(*near(0, -1), z, c),
        dev(*near(1, 1), z, c),
        dev(*near(1, -1), z, c),
        {"clip": q, "seq": (1 - ylo) * 32 + z * 2 + 1 - c},
    ]
    for p in partners:
        pl.semaphore_signal(barrier, inc=1, device_id=p, device_id_type=MESH)
    pl.semaphore_wait(barrier, len(partners))

    keep = pltpu.make_async_copy(ws.at[2 * q + c], zbuf.at[z, c], loc.at[0])
    keep.start()
    swap = pltpu.make_async_remote_copy(
        ws.at[2 * q + 1 - c], zbuf.at[z, c], swap_s, swap_r, device_id=sib, device_id_type=MESH
    )
    swap.start()
    mine = pltpu.make_async_copy(xg.at[s], own, loc.at[1])
    mine.start()
    keep.wait()
    pltpu.make_async_remote_copy(
        ws.at[2 * q + 1 - c], zbuf.at[z, 1 - c], swap_s, swap_r, device_id=sib, device_id_type=MESH
    ).wait_recv()
    mine.wait()
    put = pltpu.make_async_copy(own, r_out.at[s], loc.at[2])
    put.start()

    def zcopy(origin, step):
        o = (origin + 2 * NZ) % NZ
        return pltpu.make_async_remote_copy(
            zbuf.at[o], zbuf.at[o], zsend, zrecv.at[o],
            device_id=dev(x, y, (z + step + NZ) % NZ, c), device_id_type=MESH,
        )

    def zwait(origin):
        zcopy(origin, 1).wait_recv()

    def a2a(dist, count=4):
        zz = (z + dist + NZ) % NZ

        def one(i, carry):
            t = (i // 2) * 32 + zz * 2 + i % 2
            pltpu.make_async_remote_copy(
                xg.at[t], r_out.at[s], a_send, a_recv,
                device_id={"clip": q, "seq": t}, device_id_type=MESH,
            ).start()
            return carry

        lax.fori_loop(0, 4, one, 0)

    def a2a_home():
        for yl, cc in ((ylo, 1 - c), (1 - ylo, c), (1 - ylo, 1 - c)):
            t = yl * 32 + z * 2 + cc
            pltpu.make_async_remote_copy(
                xg.at[t], r_out.at[s], a_send, a_recv,
                device_id={"clip": q, "seq": t}, device_id_type=MESH,
            ).start()

    group = z // 4
    order = [group, (group + 1) % 4, (group + 3) % 4, (group + 2) % 4]

    def spot(u, h, xx, yy):
        off, n = HALF[h]
        at = (xx * 2 + yy // 2) * D + (yy % 2) * 576 + order[u] * UNIT + off
        return pl.multiple_of(at, 16), n

    def push(u, h, xx, yy, axis, step):
        at, n = spot(u, h, xx, yy)
        nx, ny = near(axis, step)
        pltpu.make_async_remote_copy(
            wbuf.at[pl.ds(at, n)], wbuf.at[pl.ds(at, n)], p_send,
            p_recv.at[(u * 2 + h) * 16 + xx * 4 + yy],
            device_id=dev(nx, ny, z, c), device_id_type=MESH,
        ).start()

    def deliver(u, h, xx, yy):
        at, n = spot(u, h, xx, yy)
        to = pl.multiple_of(at + (xx * 2 + yy // 2) * D + c * D, 16)
        pltpu.make_async_remote_copy(
            wbuf.at[pl.ds(at, n)], w_out.at[pl.ds(to, n)], d_send, d_recv,
            device_id=sib, device_id_type=MESH,
        ).start()
        pltpu.make_async_copy(wbuf.at[pl.ds(at, n)], w_out.at[pl.ds(to, n)], h_sem).start()

    def arrive(u, h, xx, yy):
        at, n = spot(u, h, xx, yy)
        pltpu.make_async_remote_copy(
            wbuf.at[pl.ds(at, n)], wbuf.at[pl.ds(at, n)], p_send,
            p_recv.at[(u * 2 + h) * 16 + xx * 4 + yy],
            device_id=sib, device_id_type=MESH,
        ).wait_recv()
        deliver(u, h, xx, yy)

    def cell(axis, a, b):
        if axis == 0:
            return (x + a + 4) % 4, (y + b + 4) % 4
        return (x + b + 4) % 4, (y + a + 4) % 4

    def ways(u, h):
        first = (u + h) % 2
        return first, 1 - first, (1 if (u // 2 + h) % 2 == 0 else -1)

    def launch(u):
        for t in range(3):
            parts = []
            for zi in range(4):
                for cc in range(2):
                    parts.append(zbuf[order[u] * 4 + zi, cc, 18 * t : 18 * t + 18, :].astype(F32))
            at, _ = spot(u, 0, x, y)
            wbuf[pl.ds(at, UNIT), 128 * t : 128 * t + 128] = jnp.concatenate(parts, axis=0).astype(BF16)
        for h in range(2):
            first, second, _ = ways(u, h)
            for step in (1, -1):
                push(u, h, x, y, first, step)
            for step in (1, -1):
                push(u, h, x, y, second, step)
            deliver(u, h, x, y)

    def round_one(u):
        for h in range(2):
            first, second, f = ways(u, h)
            for a in (-f, f):
                blk = cell(first, a, 0)
                arrive(u, h, *blk)
                if a == -f:
                    push(u, h, *blk, first, f)
                for step in (1, -1):
                    push(u, h, *blk, second, step)
            for b in (-f, f):
                blk = cell(first, 0, b)
                arrive(u, h, *blk)
                if b == -f:
                    push(u, h, *blk, second, f)

    def round_two(u):
        for h in range(2):
            first, second, f = ways(u, h)
            blk = cell(first, 2, 0)
            arrive(u, h, *blk)
            for step in (1, -1):
                push(u, h, *blk, second, step)
            for a in (-f, f):
                for b in (-f, f):
                    blk = cell(first, a, b)
                    arrive(u, h, *blk)
                    if b == -f:
                        push(u, h, *blk, second, f)

    def round_three(u):
        for h in range(2):
            first, second, f = ways(u, h)
            arrive(u, h, *cell(first, 0, 2))
            for b in (-f, f):
                blk = cell(first, 2, b)
                arrive(u, h, *blk)
                if b == -f:
                    push(u, h, *blk, second, f)
            for a in (-f, f):
                arrive(u, h, *cell(first, a, 2))

    def round_four(u):
        for h in range(2):
            first, _, _ = ways(u, h)
            arrive(u, h, *cell(first, 2, 2))

    for step in (1, -1, 2, -2):
        zcopy(z, step).start()
    for k in (1, 2, 3):
        for d in (2 * k - 1, 2 * k):
            zwait(z - d)
            zwait(z + d)
        zcopy(z - 2 * k, 1).start()
        zcopy(z + 2 * k, -1).start()
        zcopy(z - 2 * k, 2).start()
        if k < 3:
            zcopy(z + 2 * k, -2).start()
        if k == 1:
            a2a_home()
        for d in (2 * k - 1, 2 * k):
            a2a(d)
            a2a(-d)
        if k == 2:
            launch(0)
        if k == 3:
            round_one(0)
    zwait(z - 7)
    zwait(z + 7)
    zwait(z - 8)
    a2a(7)
    a2a(-7)
    a2a(8)
    launch(1)
    launch(2)
    round_two(0)
    launch(3)
    round_one(1)
    round_one(2)
    round_three(0)
    round_one(3)
    round_two(1)
    round_two(2)
    round_four(0)
    round_two(3)
    round_three(1)
    round_three(2)
    round_three(3)
    round_four(1)
    round_four(2)
    round_four(3)

    swap.wait_send()
    put.wait()
    pltpu.make_async_copy(xg.at[pl.ds(0, 63)], xg.at[pl.ds(0, 63)], a_send).wait()
    pltpu.make_async_copy(r_out.at[pl.ds(0, 63)], r_out.at[pl.ds(0, 63)], a_recv).wait()
    pltpu.make_async_copy(zbuf.at[pl.ds(0, 15)], zbuf.at[pl.ds(0, 15)], zsend).wait()
    sent = wbuf.at[pl.ds(0, 60 * UNIT)]
    pltpu.make_async_copy(sent, sent, p_send).wait()
    pltpu.make_async_copy(wbuf, wbuf, d_send).wait()
    half = w_out.at[pl.ds(0, 8 * D)]
    pltpu.make_async_copy(half, half, d_recv).wait()
    pltpu.make_async_copy(wbuf, half, h_sem).wait()


def gather_all(ws, xg):
    dma = pltpu.SemaphoreType.DMA
    return pl.pallas_call(
        gather_kernel,
        out_shape=(
            jax.ShapeDtypeStruct((NCH * D, CH), BF16),
            jax.ShapeDtypeStruct((64, 4, D), BF16),
        ),
        in_specs=[pl.BlockSpec(memory_space=pl.ANY)] * 2,
        out_specs=(pl.BlockSpec(memory_space=pl.ANY),) * 2,
        scratch_shapes=[
            pltpu.VMEM((NZ, 2, 54, 128), BF16),
            pltpu.VMEM((8 * D, CH), BF16),
            pltpu.VMEM((4, D), BF16),
            dma((3,)), dma, dma, dma, dma((NZ,)), dma, dma,
            dma, dma((128,)), dma, dma, dma,
        ],
        compiler_params=pltpu.CompilerParams(
            collective_id=0, has_side_effects=True, vmem_limit_bytes=40 << 20
        ),
        name="gather_all",
    )(ws, xg)


NT = (((1,), (1,)), ((), ()))
TN = (((0,), (0,)), ((), ()))
NN = (((1,), (0,)), ((), ()))


def mm(a, b, dims):
    return lax.dot_general(a, b, dims, preferred_element_type=F32)


def head_back(qh, kh, vh, gh, factor, mask):
    scores = mm(qh, kh, NT) * factor
    if mask is not None:
        scores = jnp.where(mask, scores, -jnp.inf)
    top = jnp.max(scores, axis=-1, keepdims=True)
    e = jnp.exp(scores - top)
    weights = e / jnp.sum(e, axis=-1, keepdims=True)
    grad_value = mm(weights.astype(BF16), gh, TN)
    grad_weight = mm(gh, vh, NT)
    r = jnp.sum(weights * grad_weight, axis=-1, keepdims=True)
    gs = (weights * (grad_weight - r) * factor).astype(BF16)
    grad_query = mm(gs, kh, NN)
    grad_key = mm(gs, qh, TN)
    return grad_query.astype(BF16), grad_key.astype(BF16), grad_value.astype(BF16)


def temporal_kernel(
    r_ref, w_hbm, gain_ref, bias_ref, branch_ref, sums_ref, wv, qkv_s, g_s, ga_s, dq_s, sems,
):
    head_dim = D // HEADS
    factor = 1.0 / math.sqrt(head_dim)
    copies = []
    for j in range(12):
        cp = pltpu.make_async_copy(w_hbm.at[pl.ds(j * D, D)], wv.at[pl.ds(j * D, D)], sems.at[j])
        cp.start()
        copies.append(cp)
    rows = r_ref[...].astype(F32)
    xr = rows[:, 0:2, :].reshape(128, D)
    g = rows[:, 2:4, :].reshape(128, D)
    sums_ref[4:5, :] = jnp.sum(g, axis=0, keepdims=True)
    g_s[...] = g.astype(BF16)
    mean = jnp.mean(xr, axis=-1, keepdims=True)
    centred = xr - mean
    inv_std = lax.rsqrt(jnp.mean(centred * centred, axis=-1, keepdims=True) + EPS)
    normal = centred * inv_std
    gain = gain_ref[...]
    normed = (normal * gain).astype(BF16)
    for j in range(9):
        copies[j].wait()
        qkv_s[:, CH * j : CH * j + CH] = (
            mm(normed, wv[j * D : j * D + D, :], NN) + bias_ref[:, CH * j : CH * j + CH]
        ).astype(BF16)
    acc = None
    for j in range(3):
        copies[9 + j].wait()
        part = mm(g_s[:, CH * j : CH * j + CH], wv[(9 + j) * D : (10 + j) * D, :], NT)
        acc = part if acc is None else acc + part
    ga_s[...] = acc.astype(BF16)
    ri = lax.broadcasted_iota(jnp.int32, (128, 128), 0)
    ci = lax.broadcasted_iota(jnp.int32, (128, 128), 1)
    mask = (ri & 1) == (ci & 1)
    for h in range(HEADS):
        lo, hi = h * head_dim, (h + 1) * head_dim
        gq, gk, gv = head_back(
            qkv_s[:, lo:hi], qkv_s[:, D + lo : D + hi], qkv_s[:, 2 * D + lo : 2 * D + hi],
            ga_s[:, lo:hi], factor, mask,
        )
        dq_s[:, lo:hi] = gq
        dq_s[:, D + lo : D + hi] = gk
        dq_s[:, 2 * D + lo : 2 * D + hi] = gv
    acc = None
    for j in range(9):
        part = mm(dq_s[:, CH * j : CH * j + CH], wv[j * D : j * D + D, :], NT)
        acc = part if acc is None else acc + part
    grad_normed = acc
    sums_ref[0:1, :] = jnp.sum(grad_normed * normal, axis=0, keepdims=True)
    for j in range(3):
        sums_ref[1 + j : 2 + j, :] = jnp.sum(
            dq_s[:, D * j : D * j + D].astype(F32), axis=0, keepdims=True
        )
    hat = grad_normed * gain
    branch = inv_std * (
        hat
        - jnp.mean(hat, axis=-1, keepdims=True)
        - normal * jnp.mean(hat * normal, axis=-1, keepdims=True)
    )
    branch_ref[...] = branch.reshape(64, 2, D).astype(BF16)


def temporal(r, w, gain, bias):
    vm = pl.BlockSpec(memory_space=pltpu.VMEM)
    return pl.pallas_call(
        temporal_kernel,
        out_shape=(
            jax.ShapeDtypeStruct((64, 2, D), BF16),
            jax.ShapeDtypeStruct((5, D), F32),
        ),
        in_specs=[vm, pl.BlockSpec(memory_space=pl.ANY), vm, vm],
        out_specs=(vm, vm),
        scratch_shapes=[
            pltpu.VMEM((12 * D, CH), BF16),
            pltpu.VMEM((128, 3 * D), BF16),
            pltpu.VMEM((128, D), BF16),
            pltpu.VMEM((128, D), BF16),
            pltpu.VMEM((128, 3 * D), BF16),
            pltpu.SemaphoreType.DMA((12,)),
        ],
        compiler_params=pltpu.CompilerParams(vmem_limit_bytes=48 << 20),
        name="temporal",
    )(r, w, gain, bias)


def spatial_kernel(b_ref, g_ref, qkv_ref, w_hbm, resid_ref, dqkv_ref, sums_ref, wv, ga_s, sems):
    head_dim = D // HEADS
    factor = 1.0 / math.sqrt(head_dim)
    copies = []
    for j in range(3):
        cp = pltpu.make_async_copy(
            w_hbm.at[pl.ds((12 + j) * D, D)], wv.at[pl.ds(j * D, D)], sems.at[j]
        )
        cp.start()
        copies.append(cp)
    branch = b_ref[...].astype(F32).reshape(128, D)
    resid = (g_ref[...].astype(F32) + branch).astype(BF16)
    resid_ref[...] = resid
    sums_ref[3:4, :] = jnp.sum(resid.astype(F32), axis=0, keepdims=True)
    acc = None
    for j in range(3):
        copies[j].wait()
        part = mm(resid_ref[:, CH * j : CH * j + CH], wv[j * D : j * D + D, :], NT)
        acc = part if acc is None else acc + part
    ga_s[...] = acc.astype(BF16)
    for h in range(HEADS):
        lo, hi = h * head_dim, (h + 1) * head_dim
        gq, gk, gv = head_back(
            qkv_ref[:, lo:hi], qkv_ref[:, D + lo : D + hi], qkv_ref[:, 2 * D + lo : 2 * D + hi],
            ga_s[:, lo:hi], factor, None,
        )
        dqkv_ref[:, lo:hi] = gq
        dqkv_ref[:, D + lo : D + hi] = gk
        dqkv_ref[:, 2 * D + lo : 2 * D + hi] = gv
    for j in range(3):
        sums_ref[j : j + 1, :] = jnp.sum(
            dqkv_ref[:, D * j : D * j + D].astype(F32), axis=0, keepdims=True
        )


def spatial(b, g, qkv, w):
    vm = pl.BlockSpec(memory_space=pltpu.VMEM)
    return pl.pallas_call(
        spatial_kernel,
        out_shape=(
            jax.ShapeDtypeStruct((128, D), BF16),
            jax.ShapeDtypeStruct((128, 3 * D), BF16),
            jax.ShapeDtypeStruct((4, D), F32),
        ),
        in_specs=[vm, vm, vm, pl.BlockSpec(memory_space=pl.ANY)],
        out_specs=(vm, vm, vm),
        scratch_shapes=[
            pltpu.VMEM((3 * D, CH), BF16),
            pltpu.VMEM((128, D), BF16),
            pltpu.SemaphoreType.DMA((3,)),
        ],
        compiler_params=pltpu.CompilerParams(vmem_limit_bytes=40 << 20),
        name="spatial",
    )(b, g, qkv, w)


def prepare(block_input, out_grad, qkv_weight, out_weight, spatial_out_weight):
    rows = qkv_weight.shape[0]
    pad = jnp.zeros((rows, CH), BF16)
    w = jnp.concatenate([qkv_weight, out_weight, spatial_out_weight, pad], axis=1)
    ws = w.reshape(rows, NCH, 3, 128).transpose(1, 2, 0, 3).reshape(NCH, 3 * rows, 128)
    xg = jnp.concatenate([block_input.reshape(64, 2, D), out_grad.reshape(64, 2, D)], axis=1)
    return ws, xg


def per_device(
    block_input, out_grad, spatial_qkv, norm_gain, qkv_weight, qkv_bias, out_weight,
    spatial_out_weight, grad_sums,
):
    ws, xg = prepare(block_input, out_grad, qkv_weight, out_weight, spatial_out_weight)
    w, r = gather_all(ws, xg)
    branch, sums_a = temporal(r, w, norm_gain.reshape(1, D), qkv_bias.reshape(1, 3 * D))
    back = lax.all_to_all(branch, "seq", split_axis=0, concat_axis=0, tiled=True)
    resid, sgrad, sums_b = spatial(back, out_grad.reshape(128, D), spatial_qkv.reshape(128, 3 * D), w)
    partial_sums = jnp.concatenate([sums_a, sums_b], axis=0)
    n = lax.axis_size("seq")
    blocks = jnp.moveaxis(partial_sums.reshape(9, n, D // n), 1, 0)
    share = jnp.sum(lax.all_to_all(blocks, "seq", 0, 0, tiled=True), axis=0)
    everyone = jnp.broadcast_to(share, (lax.axis_size("clip"), *share.shape))
    total = jnp.sum(lax.all_to_all(everyone, "clip", 0, 0, tiled=True), axis=0)
    tokens = 128 * lax.axis_size("seq") * lax.axis_size("clip")
    return (
        resid.reshape(1, 1, 128, D),
        sgrad.reshape(1, 1, 128, 3 * D),
        grad_sums + total * (1.0 / math.sqrt(tokens)),
    )


def solution(mesh):
    in_specs = (
        P("clip", "seq", None, None),
        P("clip", "seq", None, None),
        P("clip", "seq", None, None),
        P(),
        P("seq", None),
        P(),
        P("seq", None),
        P("seq", None),
        P(None, "seq"),
    )
    out_specs = (P("clip", "seq", None, None), P("clip", "seq", None, None), P(None, "seq"))
    return jax.shard_map(
        per_device, mesh=mesh, in_specs=in_specs, out_specs=out_specs, check_vma=False
    )
```

time: 313 us -> 171 us (0.55)
  waiting for transfers between devices: 130 us -> 0 us
  Pallas kernels: 0 us -> 100 us
  matrix products: 33.1 us -> 0 us
  local copies, waits for them, and re-layouts: 34.8 us -> 4.44 us
  starting transfers between devices: 15 us -> 0 us
  blocking collectives: 76.6 us -> 62.1 us
  between operations: 14.4 us -> 0.92 us
  other arithmetic: 8.26 us -> 2.87 us
    all_gather x1 -> x0, waiting for transfers between devices: 104 us -> none  [side_by_side(): lax.all_gather(both, axis, axis=dim, tiled=True)]
    pallas_call x0 -> x3, Pallas kernels: none -> 100 us  [the longest x1 73 us: gather_all(): pl.pallas_call(gather_kernel, out_shape=(jax.ShapeDtypeStruct((NCH * D, C...]
    dot_general x12 -> x0, matrix products: 30 us -> none  [the longest x1 5.9 us: per_device(): jnp.einsum('tc,dc->td', grad_qkv, full_qkv, preferred_element_type=jnp.fl...]
    all_to_all x2 -> x0, waiting for transfers between devices: 25.3 us -> none  [the longest x1 20.4 us: per_device(): lax.all_to_all(branch_half, 'seq', split_axis=1, concat_axis=2, tiled=True)]
    unnamed x25 -> x20, local copies, waits for them, and re-layouts: 24.6 us -> 0.81 us
    all_to_all x2 -> x0, starting transfers between devices: 14.9 us -> none  [the longest x1 8.6 us: per_device(): lax.all_to_all(branch_half, 'seq', split_axis=1, concat_axis=2, tiled=True)]
    all_to_all x2 -> x3, blocking collectives: 76.6 us -> 62.1 us  [the longest x1 32.5 us: per_device(): lax.all_to_all(branch, 'seq', split_axis=0, concat_axis=0, tiled=True)]
    reshape x4 -> x7, local copies, waits for them, and re-layouts: 6.4 us -> 2.88 us  [the longest x1 1.12 us: prepare(): block_input.reshape(64, 2, D)]
  transfers between devices with their start and end apart: 3 -> 0, of which waited for: 3 -> 0; matrix products, arithmetic and copies ran while one was open for 3% -> 0% of each run, Pallas kernels for 0% -> 0%
where the time goes in v1:
time: 171 us
  Pallas kernels  100 us (58%)
  blocking collectives  62.1 us (36%)
  local copies, waits for them, and re-layouts  4.44 us (3%)
  other arithmetic  2.87 us (2%)
    pallas_call x1, Pallas kernels, gather_all(): pl.pallas_call(gather_kernel, out_shape=(jax.ShapeDtypeStruct((NCH * D, C...  73 us
    all_to_all x1, blocking collectives, per_device(): lax.all_to_all(branch, 'seq', split_axis=0, concat_axis=0, tiled=True)  32.5 us
    all_to_all x1, blocking collectives, per_device(): share = jnp.sum(lax.all_to_all(blocks, 'seq', 0, 0, tiled=True), axis=0)  18.7 us
    pallas_call x1, Pallas kernels, temporal(): pl.pallas_call(temporal_kernel, out_shape=(jax.ShapeDtypeStruct((64, 2, D...  16.5 us
    all_to_all x1, blocking collectives, per_device(): total = jnp.sum(lax.all_to_all(everyone, 'clip', 0, 0, tiled=True), axis=0)  11 us
    pallas_call x1, Pallas kernels, spatial(): pl.pallas_call(spatial_kernel, out_shape=(jax.ShapeDtypeStruct((128, D),...  10.8 us

profile of v1, /device:TPU:1, one launch (start us, length us, event | category | flops | bytes accessed | tf_op | source)
XLA Modules:
  0.0 170.6 jit_solution(18177589153217728987)
XLA Ops:
  0.6 0.0 copy-start.2
  0.6 0.0 copy-start.4
  0.7 0.0 copy-start.3
  0.7 1.1 reshape.41
  1.8 1.1 reshape.42
  2.9 0.0 copy-start.5
  2.9 0.0 copy-start.7
  2.9 0.0 copy-done.2
  2.9 0.0 copy-done.4
  2.9 0.0 copy-done.3
  2.9 0.1 maximum_maximum_fusion
  3.0 0.3 reshape.39
  3.4 0.1 copy.22.ws
  3.5 0.1 copy-done.5
  3.6 0.0 copy-done.7
  3.6 0.6 pad_maximum_fusion.xg
  4.2 73.0 %gather_all.1 = (bf16[18432,384]{1,0:T(8,128)(2,1)}, bf16[64,4,1152]{2,1,0:T(4,128)(2,1)S(1)}) custom-call(bf16[16,54,128]{2,1,0:T(8,128)(2,1)S(1)} %copy.22.ws, bf16[64,4,1152]{2,1,0:T(4,128)(2,1)S(1)} %pad_maximum_fusion.xg), custom_call_target="tpu_custom_call" | custom-call | tf_op jit(solution)/shard_map/gather_all/pallas_call | solution.py:283
  77.2 0.0 copy-start
  77.2 0.0 copy-start.1
  77.3 16.5 %temporal.1 = (bf16[64,2,1152]{2,1,0:T(2,128)(2,1)S(1)}, f32[5,1152]{1,0:T(8,128)S(1)}) custom-call(bf16[64,4,1152]{2,1,0:T(4,128)(2,1)S(1)} %get-tuple-element.10.r_ref, bf16[18432,384]{1,0:T(8,128)(2,1)} %get-tuple-element.11.w_hbm, f32[1,1152]{1,0:T(1,128)S(1)} %reshape.43.gain_ref, f32[1,3456]{1,0:T(1,128)S(1)} %reshape.44.bias_ref), custom_call_target="tpu_custom_call" | custom-call | tf_op jit(solution)/shard_map/temporal/pallas_call | solution.py:395
  93.7 32.5 %all_to_all.15.b_ref = bf16[64,2,1152]{2,1,0:T(2,128)(2,1)S(1)} all-to-all(bf16[64,2,1152]{2,1,0:T(2,128)(2,1)S(1)} %get-tuple-element.12), channel_id=1, replica_groups=mesh['seq'=64,'clip'=8] {'seq'}, dimensions={0} | all-to-all | bytes 589824 | tf_op jit(solution)/shard_map/all_to_all | solution.py:488
  126.2 0.0 copy-done
  126.2 0.0 copy-done.1
  126.2 10.8 %spatial.1 = (bf16[128,1152]{1,0:T(8,128)(2,1)}, bf16[128,3456]{1,0:T(8,128)(2,1)}, f32[4,1152]{1,0:T(4,128)S(1)}) custom-call(bf16[64,2,1152]{2,1,0:T(2,128)(2,1)S(1)} %all_to_all.15.b_ref, bf16[128,1152]{1,0:T(8,128)(2,1)S(1)} %bitcast.11, bf16[128,3456]{1,0:T(8,128)(2,1)S(1)} %bitcast.12, bf16[18432,384]{1,0:T(8,128)(2,1)} %get-tuple-element.11.w_hbm), custom_call_target="tpu_custom_call" | custom-call | tf_op jit(solution)/shard_map/spatial/pallas_call | solution.py:453
  137.0 0.3 reshape.49
  137.3 0.2 copy.23
  137.5 0.0 copy-start.6
  137.5 0.3 reshape.50
  137.8 18.7 %all_to_all.16 = f32[64,1,162]{2,1,0:T(1,128)S(1)} all-to-all(f32[64,1,162]{2,1,0:T(1,128)S(1)} %reshape.50), channel_id=1, replica_groups=mesh['seq'=64,'clip'=8] {'seq'}, dimensions={0} | all-to-all | bytes 82944 | tf_op jit(solution)/shard_map/all_to_all | solution.py:493
  156.5 0.5 broadcast.2
  157.0 0.8 reduce
  157.8 0.2 reshape.51
  158.0 0.1 reduce_sum.18
  158.1 0.1 reshape.52
  158.2 11.0 %all_to_all.17 = f32[8,1,162]{2,1,0:T(1,128)S(1)} all-to-all(f32[8,1,162]{2,1,0:T(1,128)S(1)} %reshape.52), channel_id=1, replica_groups=mesh['seq'=64,'clip'=8] {'clip'}, dimensions={0} | all-to-all | bytes 10368 | tf_op jit(solution)/shard_map/all_to_all | solution.py:495
  169.2 0.7 reduce.1
  169.9 0.1 reshape.53
  170.0 0.0 copy-done.6
  170.0 0.6 multiply_add_fusion
  (8 shorter events, 0.1 us)
Async XLA Ops:
  0.6 2.3 %copy-start.2 = (bf16[18,3456]{1,0:T(8,128)(2,1)S(1)}, bf16[18,3456]{1,0:T(8,128)(2,1)}, u32[]{:S(2)}) copy-start(bf16[18,3456]{1,0:T(8,128)(2,1)} %param.13) | copy-start | bytes 373252
  0.6 2.3 %copy-start.4 = (bf16[18,1152]{1,0:T(8,128)(2,1)S(1)}, bf16[18,1152]{1,0:T(8,128)(2,1)}, u32[]{:S(2)}) copy-start(bf16[18,1152]{1,0:T(8,128)(2,1)} %param.15) | copy-start | bytes 124420
  0.7 2.3 %copy-start.3 = (bf16[18,1152]{1,0:T(8,128)(2,1)S(1)}, bf16[18,1152]{1,0:T(8,128)(2,1)}, u32[]{:S(2)}) copy-start(bf16[18,1152]{1,0:T(8,128)(2,1)} %param.16) | copy-start | bytes 124420
  2.9 0.7 copy-start.5
  2.9 0.7 copy-start.7
  77.2 49.0 %copy-start = (bf16[1,1,128,1152]{3,2,1,0:T(8,128)(2,1)S(1)}, bf16[1,1,128,1152]{3,2,1,0:T(8,128)(2,1)}, u32[]{:S(2)}) copy-start(bf16[1,1,128,1152]{3,2,1,0:T(8,128)(2,1)} %param.10) | copy-start | bytes 884740
  77.2 49.0 %copy-start.1 = (bf16[1,1,128,3456]{3,2,1,0:T(8,128)(2,1)S(1)}, bf16[1,1,128,3456]{3,2,1,0:T(8,128)(2,1)}, u32[]{:S(2)}) copy-start(bf16[1,1,128,3456]{3,2,1,0:T(8,128)(2,1)} %param.11) | copy-start | bytes 2654212
  137.5 32.4 %copy-start.6 = (f32[9,18]{1,0:T(8,128)S(1)}, f32[9,18]{1,0:T(8,128)}, u32[]{:S(2)}) copy-start(f32[9,18]{1,0:T(8,128)} %param.17) | copy-start | bytes 1948

commit v2 on v1

--- a/solution.py
+++ b/solution.py
@@ -311,13 +311,16 @@
     return lax.dot_general(a, b, dims, preferred_element_type=F32)
 
 
-def head_back(qh, kh, vh, gh, factor, mask):
+def softmax_of(qh, kh, factor, mask):
     scores = mm(qh, kh, NT) * factor
     if mask is not None:
         scores = jnp.where(mask, scores, -jnp.inf)
     top = jnp.max(scores, axis=-1, keepdims=True)
     e = jnp.exp(scores - top)
-    weights = e / jnp.sum(e, axis=-1, keepdims=True)
+    return e / jnp.sum(e, axis=-1, keepdims=True)
+
+
+def grads_of(weights, qh, kh, vh, gh, factor):
     grad_value = mm(weights.astype(BF16), gh, TN)
     grad_weight = mm(gh, vh, NT)
     r = jnp.sum(weights * grad_weight, axis=-1, keepdims=True)
@@ -327,20 +330,45 @@
     return grad_query.astype(BF16), grad_key.astype(BF16), grad_value.astype(BF16)
 
 
-def temporal_kernel(
-    r_ref, w_hbm, gain_ref, bias_ref, branch_ref, sums_ref, wv, qkv_s, g_s, ga_s, dq_s, sems,
+def rest_kernel(
+    tokens, r_ref, w_hbm, gain_ref, bias_ref, og_ref, sq_ref, gsum_ref, resid_ref, dqkv_ref, tot_ref,
+    wv, qkv_s, g_s, ga_s, dq_s, sw_s, bsrc, brecv, sums, mate, slab, zin, pin, fin,
+    wsem, b_send, b_recv, m_send, m_recv, z_send, z_recv, p_send, p_recv, f_send, f_recv,
 ):
+    x, y, z, c = place()
+    s, q = lax.axis_index("seq"), lax.axis_index("clip")
+    sib = dev(x, y, z, 1 - c)
+    barrier = pltpu.get_barrier_semaphore()
+
+    def greet_seq(i, carry):
+        pl.semaphore_signal(
+            barrier, inc=1, device_id={"clip": q, "seq": (s + i) % 64}, device_id_type=MESH
+        )
+        return carry
+
+    def xy_peer(i):
+        return (x + i // 4) % 4, (y + i % 4) % 4
+
+    def greet_xy(i, carry):
+        pl.semaphore_signal(barrier, inc=1, device_id=dev(*xy_peer(i), z, c), device_id_type=MESH)
+        return carry
+
+    lax.fori_loop(1, 64, greet_seq, 0)
+    lax.fori_loop(1, 16, greet_xy, 0)
+
+    sums[8:16, :] = jnp.zeros((8, D), F32)
+    slab[...] = jnp.zeros((NZ, 8, 128), F32)
     head_dim = D // HEADS
     factor = 1.0 / math.sqrt(head_dim)
     copies = []
-    for j in range(12):
-        cp = pltpu.make_async_copy(w_hbm.at[pl.ds(j * D, D)], wv.at[pl.ds(j * D, D)], sems.at[j])
+    for j in range(15):
+        cp = pltpu.make_async_copy(w_hbm.at[pl.ds(j * D, D)], wv.at[pl.ds(j * D, D)], wsem.at[j])
         cp.start()
         copies.append(cp)
     rows = r_ref[...].astype(F32)
     xr = rows[:, 0:2, :].reshape(128, D)
     g = rows[:, 2:4, :].reshape(128, D)
-    sums_ref[4:5, :] = jnp.sum(g, axis=0, keepdims=True)
+    sums[4:5, :] = jnp.sum(g, axis=0, keepdims=True)
     g_s[...] = g.astype(BF16)
     mean = jnp.mean(xr, axis=-1, keepdims=True)
     centred = xr - mean
@@ -364,9 +392,10 @@
     mask = (ri & 1) == (ci & 1)
     for h in range(HEADS):
         lo, hi = h * head_dim, (h + 1) * head_dim
-        gq, gk, gv = head_back(
-            qkv_s[:, lo:hi], qkv_s[:, D + lo : D + hi], qkv_s[:, 2 * D + lo : 2 * D + hi],
-            ga_s[:, lo:hi], factor, mask,
+        qh, kh = qkv_s[:, lo:hi], qkv_s[:, D + lo : D + hi]
+        gq, gk, gv = grads_of(
+            softmax_of(qh, kh, factor, mask), qh, kh, qkv_s[:, 2 * D + lo : 2 * D + hi],
+            ga_s[:, lo:hi], factor,
         )
         dq_s[:, lo:hi] = gq
         dq_s[:, D + lo : D + hi] = gk
@@ -376,97 +405,161 @@
         part = mm(dq_s[:, CH * j : CH * j + CH], wv[j * D : j * D + D, :], NT)
         acc = part if acc is None else acc + part
     grad_normed = acc
-    sums_ref[0:1, :] = jnp.sum(grad_normed * normal, axis=0, keepdims=True)
-    for j in range(3):
-        sums_ref[1 + j : 2 + j, :] = jnp.sum(
-            dq_s[:, D * j : D * j + D].astype(F32), axis=0, keepdims=True
-        )
     hat = grad_normed * gain
     branch = inv_std * (
         hat
         - jnp.mean(hat, axis=-1, keepdims=True)
         - normal * jnp.mean(hat * normal, axis=-1, keepdims=True)
     )
-    branch_ref[...] = branch.reshape(64, 2, D).astype(BF16)
-
-
-def temporal(r, w, gain, bias):
-    vm = pl.BlockSpec(memory_space=pltpu.VMEM)
-    return pl.pallas_call(
-        temporal_kernel,
-        out_shape=(
-            jax.ShapeDtypeStruct((64, 2, D), BF16),
-            jax.ShapeDtypeStruct((5, D), F32),
-        ),
-        in_specs=[vm, pl.BlockSpec(memory_space=pl.ANY), vm, vm],
-        out_specs=(vm, vm),
-        scratch_shapes=[
-            pltpu.VMEM((12 * D, CH), BF16),
-            pltpu.VMEM((128, 3 * D), BF16),
-            pltpu.VMEM((128, D), BF16),
-            pltpu.VMEM((128, D), BF16),
-            pltpu.VMEM((128, 3 * D), BF16),
-            pltpu.SemaphoreType.DMA((12,)),
-        ],
-        compiler_params=pltpu.CompilerParams(vmem_limit_bytes=48 << 20),
-        name="temporal",
-    )(r, w, gain, bias)
-
-
-def spatial_kernel(b_ref, g_ref, qkv_ref, w_hbm, resid_ref, dqkv_ref, sums_ref, wv, ga_s, sems):
-    head_dim = D // HEADS
-    factor = 1.0 / math.sqrt(head_dim)
-    copies = []
+    bsrc[...] = branch.reshape(64, 2, D).astype(BF16)
+
+    pl.semaphore_wait(barrier, 78)
+    ylo = s // 32
+    for dz in (8, 7, 9, 6, 10, 5, 11, 4, 12, 3, 13, 2, 14, 1, 15):
+        zz = (z + dz) % NZ
+
+        def back(i, carry):
+            t = ((ylo + i // 2) % 2) * 32 + zz * 2 + (c + i) % 2
+            pltpu.make_async_remote_copy(
+                bsrc.at[t], brecv.at[s], b_send, b_recv,
+                device_id={"clip": q, "seq": t}, device_id_type=MESH,
+            ).start()
+            return carry
+
+        lax.fori_loop(0, 4, back, 0)
+    for yl, cc in ((1 - ylo, c), (1 - ylo, 1 - c), (ylo, 1 - c)):
+        t = yl * 32 + z * 2 + cc
+        pltpu.make_async_remote_copy(
+            bsrc.at[t], brecv.at[s], b_send, b_recv,
+            device_id={"clip": q, "seq": t}, device_id_type=MESH,
+        ).start()
+    brecv[s] = bsrc[s]
+
+    sums[0:1, :] = jnp.sum(grad_normed * normal, axis=0, keepdims=True)
     for j in range(3):
-        cp = pltpu.make_async_copy(
-            w_hbm.at[pl.ds((12 + j) * D, D)], wv.at[pl.ds(j * D, D)], sems.at[j]
+        sums[1 + j : 2 + j, :] = jnp.sum(
+            dq_s[:, D * j : D * j + D].astype(F32), axis=0, keepdims=True
         )
-        cp.start()
-        copies.append(cp)
-    branch = b_ref[...].astype(F32).reshape(128, D)
-    resid = (g_ref[...].astype(F32) + branch).astype(BF16)
+    for h in range(HEADS):
+        lo, hi = h * head_dim, (h + 1) * head_dim
+        sw_s[h] = softmax_of(sq_ref[:, lo:hi], sq_ref[:, D + lo : D + hi], factor, None)
+    for j in range(12, 15):
+        copies[j].wait()
+
+    pltpu.make_async_copy(brecv.at[pl.ds(0, 63)], brecv.at[pl.ds(0, 63)], b_recv).wait()
+    resid = (og_ref[...].astype(F32) + brecv[...].astype(F32).reshape(128, D)).astype(BF16)
     resid_ref[...] = resid
-    sums_ref[3:4, :] = jnp.sum(resid.astype(F32), axis=0, keepdims=True)
+    sums[8:9, :] = jnp.sum(resid.astype(F32), axis=0, keepdims=True)
     acc = None
     for j in range(3):
-        copies[j].wait()
-        part = mm(resid_ref[:, CH * j : CH * j + CH], wv[j * D : j * D + D, :], NT)
+        part = mm(resid_ref[:, CH * j : CH * j + CH], wv[(12 + j) * D : (13 + j) * D, :], NT)
         acc = part if acc is None else acc + part
     ga_s[...] = acc.astype(BF16)
     for h in range(HEADS):
         lo, hi = h * head_dim, (h + 1) * head_dim
-        gq, gk, gv = head_back(
-            qkv_ref[:, lo:hi], qkv_ref[:, D + lo : D + hi], qkv_ref[:, 2 * D + lo : 2 * D + hi],
-            ga_s[:, lo:hi], factor, None,
+        gq, gk, gv = grads_of(
+            sw_s[h], sq_ref[:, lo:hi], sq_ref[:, D + lo : D + hi],
+            sq_ref[:, 2 * D + lo : 2 * D + hi], ga_s[:, lo:hi], factor,
         )
         dqkv_ref[:, lo:hi] = gq
         dqkv_ref[:, D + lo : D + hi] = gk
         dqkv_ref[:, 2 * D + lo : 2 * D + hi] = gv
     for j in range(3):
-        sums_ref[j : j + 1, :] = jnp.sum(
+        sums[5 + j : 6 + j, :] = jnp.sum(
             dqkv_ref[:, D * j : D * j + D].astype(F32), axis=0, keepdims=True
         )
 
-
-def spatial(b, g, qkv, w):
+    swap = pltpu.make_async_remote_copy(
+        sums, mate, m_send, m_recv, device_id=sib, device_id_type=MESH
+    )
+    swap.start()
+    swap.wait_recv()
+    both = sums[...] + mate[...]
+    mine = jnp.where(c == 0, both[0:8], jnp.concatenate([both[5:9], both[9:13]], axis=0))
+    for k in range(NZ):
+        for yl in range(2):
+            lo = yl * 576 + 36 * k
+            slab[k, :, 36 * yl : 36 * yl + 36] = mine[:, lo : lo + 36]
+
+    def zsend(i, carry):
+        k = (z + i) % NZ
+        pltpu.make_async_remote_copy(
+            slab.at[k], zin.at[z], z_send, z_recv, device_id=dev(x, y, k, c), device_id_type=MESH
+        ).start()
+        return carry
+
+    def psend(i, carry):
+        pltpu.make_async_remote_copy(
+            zin.at[NZ], pin.at[x * 4 + y], p_send, p_recv,
+            device_id=dev(*xy_peer(i), z, c), device_id_type=MESH,
+        ).start()
+        return carry
+
+    lax.fori_loop(1, 16, zsend, 0)
+    zin[z] = slab[z]
+    pltpu.make_async_copy(zin.at[pl.ds(0, 15)], zin.at[pl.ds(0, 15)], z_recv).wait()
+    zsum = jnp.sum(zin[0:NZ], axis=0)
+    zin[NZ] = zsum
+    lax.fori_loop(1, 16, psend, 0)
+    pin[x * 4 + y] = zsum
+    pltpu.make_async_copy(pin.at[pl.ds(0, 15)], pin.at[pl.ds(0, 15)], p_recv).wait()
+    psum = jnp.sum(pin[...], axis=0)
+    fin[c] = psum
+    last = pltpu.make_async_remote_copy(
+        fin.at[c], fin.at[c], f_send, f_recv, device_id=sib, device_id_type=MESH
+    )
+    last.start()
+    pltpu.make_async_remote_copy(
+        fin.at[c], fin.at[1 - c], f_send, f_recv, device_id=sib, device_id_type=MESH
+    ).wait_recv()
+    total = jnp.concatenate([fin[0, 0:5], fin[1, 0:4]], axis=0)
+    part = ylo * 2 + c
+    pick = total[:, 0:18]
+    for k in range(1, 4):
+        pick = jnp.where(part == k, total[:, 18 * k : 18 * k + 18], pick)
+    tot_ref[...] = gsum_ref[...] + pick * (1.0 / math.sqrt(tokens))
+
+    swap.wait_send()
+    last.wait_send()
+    pltpu.make_async_copy(bsrc.at[pl.ds(0, 63)], bsrc.at[pl.ds(0, 63)], b_send).wait()
+    pltpu.make_async_copy(slab.at[pl.ds(0, 15)], slab.at[pl.ds(0, 15)], z_send).wait()
+    pltpu.make_async_copy(pin.at[pl.ds(0, 15)], pin.at[pl.ds(0, 15)], p_send).wait()
+
+
+def rest(r, w, gain, bias, og, sq, gsum, tokens):
     vm = pl.BlockSpec(memory_space=pltpu.VMEM)
+    dma = pltpu.SemaphoreType.DMA
     return pl.pallas_call(
-        spatial_kernel,
+        functools.partial(rest_kernel, tokens),
         out_shape=(
             jax.ShapeDtypeStruct((128, D), BF16),
             jax.ShapeDtypeStruct((128, 3 * D), BF16),
-            jax.ShapeDtypeStruct((4, D), F32),
+            jax.ShapeDtypeStruct((9, D // 64), F32),
         ),
-        in_specs=[vm, vm, vm, pl.BlockSpec(memory_space=pl.ANY)],
+        in_specs=[vm, pl.BlockSpec(memory_space=pl.ANY), vm, vm, vm, vm, vm],
         out_specs=(vm, vm, vm),
         scratch_shapes=[
-            pltpu.VMEM((3 * D, CH), BF16),
+            pltpu.VMEM((15 * D, CH), BF16),
+            pltpu.VMEM((128, 3 * D), BF16),
             pltpu.VMEM((128, D), BF16),
-            pltpu.SemaphoreType.DMA((3,)),
+            pltpu.VMEM((128, D), BF16),
+            pltpu.VMEM((128, 3 * D), BF16),
+            pltpu.VMEM((HEADS, 128, 128), F32),
+            pltpu.VMEM((64, 2, D), BF16),
+            pltpu.VMEM((64, 2, D), BF16),
+            pltpu.VMEM((16, D), F32),
+            pltpu.VMEM((16, D), F32),
+            pltpu.VMEM((NZ, 8, 128), F32),
+            pltpu.VMEM((NZ + 1, 8, 128), F32),
+            pltpu.VMEM((16, 8, 128), F32),
+            pltpu.VMEM((2, 8, 128), F32),
+            dma((15,)), dma, dma, dma, dma, dma, dma, dma, dma, dma, dma,
         ],
-        compiler_params=pltpu.CompilerParams(vmem_limit_bytes=40 << 20),
-        name="spatial",
-    )(b, g, qkv, w)
+        compiler_params=pltpu.CompilerParams(
+            collective_id=1, has_side_effects=True, vmem_limit_bytes=56 << 20
+        ),
+        name="rest",
+    )(r, w, gain, bias, og, sq, gsum)
 
 
 def prepare(block_input, out_grad, qkv_weight, out_weight, spatial_out_weight):
@@ -484,21 +577,12 @@
 ):
     ws, xg = prepare(block_input, out_grad, qkv_weight, out_weight, spatial_out_weight)
     w, r = gather_all(ws, xg)
-    branch, sums_a = temporal(r, w, norm_gain.reshape(1, D), qkv_bias.reshape(1, 3 * D))
-    back = lax.all_to_all(branch, "seq", split_axis=0, concat_axis=0, tiled=True)
-    resid, sgrad, sums_b = spatial(back, out_grad.reshape(128, D), spatial_qkv.reshape(128, 3 * D), w)
-    partial_sums = jnp.concatenate([sums_a, sums_b], axis=0)
-    n = lax.axis_size("seq")
-    blocks = jnp.moveaxis(partial_sums.reshape(9, n, D // n), 1, 0)
-    share = jnp.sum(lax.all_to_all(blocks, "seq", 0, 0, tiled=True), axis=0)
-    everyone = jnp.broadcast_to(share, (lax.axis_size("clip"), *share.shape))
-    total = jnp.sum(lax.all_to_all(everyone, "clip", 0, 0, tiled=True), axis=0)
     tokens = 128 * lax.axis_size("seq") * lax.axis_size("clip")
-    return (
-        resid.reshape(1, 1, 128, D),
-        sgrad.reshape(1, 1, 128, 3 * D),
-        grad_sums + total * (1.0 / math.sqrt(tokens)),
+    resid, sgrad, totals = rest(
+        r, w, norm_gain.reshape(1, D), qkv_bias.reshape(1, 3 * D), out_grad.reshape(128, D),
+        spatial_qkv.reshape(128, 3 * D), grad_sums, tokens,
     )
+    return resid.reshape(1, 1, 128, D), sgrad.reshape(1, 1, 128, 3 * D), totals
 
 
 def solution(mesh):

time: 171 us -> 143 us (0.84)
  blocking collectives: 62.1 us -> 0 us
  Pallas kernels: 100 us -> 131 us
  local copies, waits for them, and re-layouts: 4.44 us -> 8.96 us
    all_to_all x3 -> x0, blocking collectives: 62.1 us -> none  [the longest x1 32.5 us: per_device(): lax.all_to_all(branch, 'seq', split_axis=0, concat_axis=0, tiled=True)]
    pallas_call x2 -> x1, Pallas kernels: 27.2 us -> 58.5 us  [rest(): pl.pallas_call(functools.partial(rest_kernel, tokens), out_shape=(jax.Sha...]
    unnamed x20 -> x11, local copies, waits for them, and re-layouts: 0.81 us -> 5.64 us
where the time goes in v2:
time: 143 us
  Pallas kernels  131 us (92%)
  local copies, waits for them, and re-layouts  8.96 us (6%)
  other arithmetic  1.66 us (1%)
    pallas_call x1, Pallas kernels, gather_all(): pl.pallas_call(gather_kernel, out_shape=(jax.ShapeDtypeStruct((NCH * D, C...  73 us
    pallas_call x1, Pallas kernels, rest(): pl.pallas_call(functools.partial(rest_kernel, tokens), out_shape=(jax.Sha...  58.5 us
    unnamed x11, local copies, waits for them, and re-layouts  5.64 us

profile of v2, /device:TPU:1, one launch (start us, length us, event | category | flops | bytes accessed | tf_op | source)
XLA Modules:
  0.0 142.8 jit_solution(6624322116234072412)
XLA Ops:
  0.6 0.0 copy-start.2
  0.6 1.3 reshape.40.gain_ref
  2.0 1.3 reshape.41.bias_ref
  3.3 1.0 maximum_maximum_fusion
  4.4 0.0 copy-start.1
  4.4 0.3 reshape.36
  4.8 0.1 copy.14.ws
  4.8 0.0 copy-done.2
  4.8 0.1 reshape.38
  5.0 0.4 copy-done.1
  5.3 0.1 reshape.39
  5.4 0.6 pad_maximum_fusion.xg
  6.1 73.0 %gather_all.1 = (bf16[18432,384]{1,0:T(8,128)(2,1)}, bf16[64,4,1152]{2,1,0:T(4,128)(2,1)S(1)}) custom-call(bf16[16,54,128]{2,1,0:T(8,128)(2,1)S(1)} %copy.14.ws, bf16[64,4,1152]{2,1,0:T(4,128)(2,1)S(1)} %pad_maximum_fusion.xg), custom_call_target="tpu_custom_call" | custom-call | tf_op jit(solution)/shard_map/gather_all/pallas_call | solution.py:283
  79.1 0.0 copy-start
  79.1 0.8 copy-done
  79.9 58.5 %rest.1 = (bf16[128,1152]{1,0:T(8,128)(2,1)}, bf16[128,3456]{1,0:T(8,128)(2,1)}, f32[9,18]{1,0:T(8,128)}) custom-call(bf16[64,4,1152]{2,1,0:T(4,128)(2,1)} %copy-done, bf16[18432,384]{1,0:T(8,128)(2,1)} %get-tuple-element.9.w_hbm, f32[1,1152]{1,0:T(1,128)} %reshape.40.gain_ref, f32[1,3456]{1,0:T(1,128)} %reshape.41.bias_ref, bf16[128,1152]{1,0:T(8,128)(2,1)} %bitcast.11, ...), custom_call_target="tpu_custom_call" | custom-call | tf_op jit(solution)/shard_map/rest/pallas_call | solution.py:532
  138.4 0.0 copy-start.3
  138.4 1.7 %copy.18 = bf16[1,1,128,1152]{3,2,1,0:T(8,128)(2,1)} copy(bf16[1,1,128,1152]{3,2,1,0:T(8,128)(2,1)} %bitcast.15) | data formatting | bytes 589824
  140.1 2.1 %copy.19 = bf16[1,1,128,3456]{3,2,1,0:T(8,128)(2,1)} copy(bf16[1,1,128,3456]{3,2,1,0:T(8,128)(2,1)} %bitcast.12) | data formatting | bytes 1769472
  142.2 0.0 copy-done.3
  142.2 0.6 copy.20
  (3 shorter events, 0.0 us)
Async XLA Ops:
  0.6 4.2 %copy-start.2 = (bf16[1,1,128,1152]{3,2,1,0:T(8,128)(2,1)S(1)}, bf16[1,1,128,1152]{3,2,1,0:T(8,128)(2,1)}, u32[]{:S(2)}) copy-start(bf16[1,1,128,1152]{3,2,1,0:T(8,128)(2,1)} %param.9) | copy-start | bytes 884740
  4.4 1.0 copy-start.1
  79.1 0.8 copy-start
  138.4 3.9 %copy-start.3 = (f32[9,18]{1,0:T(8,128)S(1)}, f32[9,18]{1,0:T(8,128)}, u32[]{:S(2)}) copy-start(f32[9,18]{1,0:T(8,128)} %get-tuple-element.18) | copy-start | bytes 1948

commit v3 on v2

v3 whole, which is shorter than its diff:
```python
import functools
import math

import jax
import jax.numpy as jnp
from jax import lax
from jax.experimental import pallas as pl
from jax.experimental.pallas import tpu as pltpu
from jax.sharding import PartitionSpec as P

HEADS = 16
EPS = 1e-06
MESH = pl.DeviceIdType.MESH
F32 = jnp.float32
BF16 = jnp.bfloat16

D = 1152
CH = 384
NCH = 16
NZ = 16
UNIT = 144
HALF = ((0, 80), (80, 64))


def dev(x, y, z, c):
    return {"clip": x * 2 + y // 2, "seq": (y % 2) * 32 + z * 2 + c}


def place():
    s, q = lax.axis_index("seq"), lax.axis_index("clip")
    x = q // 2
    y = (q % 2) * 2 + s // 32
    z = (s // 2) % 16
    c = s % 2
    return x, y, z, c


NT = (((1,), (1,)), ((), ()))
TN = (((0,), (0,)), ((), ()))
NN = (((1,), (0,)), ((), ()))


def mm(a, b, dims):
    return lax.dot_general(a, b, dims, preferred_element_type=F32)


def softmax_of(qh, kh, factor, mask):
    scores = mm(qh, kh, NT) * factor
    if mask is not None:
        scores = jnp.where(mask, scores, -jnp.inf)
    top = jnp.max(scores, axis=-1, keepdims=True)
    e = jnp.exp(scores - top)
    return e / jnp.sum(e, axis=-1, keepdims=True)


def grads_of(weights, qh, kh, vh, gh, factor):
    grad_value = mm(weights.astype(BF16), gh, TN)
    grad_weight = mm(gh, vh, NT)
    r = jnp.sum(weights * grad_weight, axis=-1, keepdims=True)
    gs = (weights * (grad_weight - r) * factor).astype(BF16)
    grad_query = mm(gs, kh, NN)
    grad_key = mm(gs, qh, TN)
    return grad_query.astype(BF16), grad_key.astype(BF16), grad_value.astype(BF16)


WIDE = 640


def sizes(rows):
    return pl.ds(0, rows)


def block_kernel(
    tokens, ws, x_ref, g_ref, sq_ref, gain_ref, bias_ref, gsum_ref, resid_ref, dqkv_ref, tot_ref,
    zbuf, wbuf, asrc, abuf, qkv_s, ga_s, dq_s, sw_s, bsrc, brecv, sums, mate, slab, zin, pin, fin,
    loc, swap_s, swap_r, zg_send, zg_recv, a_send, a_recv, p_send, p_recv, d_send, d_recv,
    b_send, b_recv, m_send, m_recv, z_send, z_recv, q_send, q_recv, f_send, f_recv,
):
    x, y, z, c = place()
    s, q = lax.axis_index("seq"), lax.axis_index("clip")
    ylo = s // 32
    sib = dev(x, y, z, 1 - c)

    def near(axis, step):
        if axis == 0:
            return (x + step + 4) % 4, y
        return x, (y + step + 4) % 4

    def on_line(step):
        return jnp.logical_and(z + step >= 0, z + step < NZ)

    barrier = pltpu.get_barrier_semaphore()
    partners = [
        sib,
        dev(*near(0, 1), z, c),
        dev(*near(0, -1), z, c),
        dev(*near(1, 1), z, c),
        dev(*near(1, -1), z, c),
        {"clip": q, "seq": (1 - ylo) * 32 + z * 2 + 1 - c},
    ]
    for p in partners:
        pl.semaphore_signal(barrier, inc=1, device_id=p, device_id_type=MESH)
    expected = jnp.int32(len(partners))
    for step in (1, -1, 2, -2):
        ok = on_line(step)
        expected = expected + jnp.where(ok, 1, 0)

        @pl.when(ok)
        def _():
            pl.semaphore_signal(
                barrier, inc=1, device_id=dev(x, y, (z + step + NZ) % NZ, c), device_id_type=MESH
            )

    keep = pltpu.make_async_copy(ws.at[2 * q + c], zbuf.at[z, c], loc)
    keep.start()
    sums[...] = jnp.zeros((16, D), F32)
    slab[...] = jnp.zeros((NZ, 8, 128), F32)
    pl.semaphore_wait(barrier, expected)

    swap = pltpu.make_async_remote_copy(
        ws.at[2 * q + 1 - c], zbuf.at[z, c], swap_s, swap_r, device_id=sib, device_id_type=MESH
    )
    swap.start()
    keep.wait()
    pltpu.make_async_remote_copy(
        ws.at[2 * q + 1 - c], zbuf.at[z, 1 - c], swap_s, swap_r, device_id=sib, device_id_type=MESH
    ).wait_recv()

    def zcopy(origin, step):
        o = (origin + 2 * NZ) % NZ
        kind = (0 if abs(step) == 1 else 2) + (0 if step > 0 else 1)
        return pltpu.make_async_remote_copy(
            zbuf.at[o], zbuf.at[o], zg_send.at[kind * NZ + o], zg_recv.at[o],
            device_id=dev(x, y, (z + step + NZ) % NZ, c), device_id_type=MESH,
        )

    def zforward(back, step):
        @pl.when(jnp.logical_and(on_line(back), on_line(step)))
        def _():
            zcopy(z + back, step).start()

    def zwait(back):
        @pl.when(on_line(back))
        def _():
            zcopy(z + back, 1).wait_recv()

    for step in (1, -1, 2, -2):
        zforward(0, step)

    x3 = x_ref[...].astype(F32).reshape(64, 2, D)
    g3 = g_ref[...].astype(F32).reshape(64, 2, D)
    for p in range(2):
        asrc[64 * p : 64 * p + 64] = jnp.concatenate(
            [x3[:, p : p + 1, :], g3[:, p : p + 1, :]], axis=1
        ).astype(BF16)

    def exchange(p, dist):
        @pl.when(on_line(dist))
        def _():
            zz = (z + dist + NZ) % NZ

            def one(i, carry):
                t = ((ylo + i // 2) % 2) * 32 + zz * 2 + (c + i) % 2
                pltpu.make_async_remote_copy(
                    asrc.at[64 * p + t], abuf.at[64 * p + s], a_send, a_recv.at[p],
                    device_id={"clip": q, "seq": t}, device_id_type=MESH,
                ).start()
                return carry

            lax.fori_loop(0, 4, one, 0)

    def exchange_home(p):
        for yl, cc in ((1 - ylo, c), (1 - ylo, 1 - c), (ylo, 1 - c)):
            t = yl * 32 + z * 2 + cc
            pltpu.make_async_remote_copy(
                asrc.at[64 * p + t], abuf.at[64 * p + s], a_send, a_recv.at[p],
                device_id={"clip": q, "seq": t}, device_id_type=MESH,
            ).start()
        abuf[64 * p + s] = asrc[64 * p + s]

    group = z // 4
    order = [group, group + 1 - 2 * (group % 2), 2 - group // 2, 3 - 3 * (group // 2)]

    def spot(u, h, xx, yy):
        off, n = HALF[h]
        at = (2 * (xx * 2 + yy // 2) + c) * D + (yy % 2) * 576 + order[u] * UNIT + off
        return pl.ds(pl.multiple_of(at, 16), n)

    def push(u, h, xx, yy, axis, step):
        rows = spot(u, h, xx, yy)
        nx, ny = near(axis, step)
        pltpu.make_async_remote_copy(
            wbuf.at[rows], wbuf.at[rows], p_send, p_recv.at[(u * 2 + h) * 16 + xx * 4 + yy],
            device_id=dev(nx, ny, z, c), device_id_type=MESH,
        ).start()

    def deliver(u, h, xx, yy):
        rows = spot(u, h, xx, yy)
        pltpu.make_async_remote_copy(
            wbuf.at[rows], wbuf.at[rows], d_send, d_recv, device_id=sib, device_id_type=MESH
        ).start()

    def arrive(u, h, xx, yy):
        rows = spot(u, h, xx, yy)
        pltpu.make_async_remote_copy(
            wbuf.at[rows], wbuf.at[rows], p_send, p_recv.at[(u * 2 + h) * 16 + xx * 4 + yy],
            device_id=sib, device_id_type=MESH,
        ).wait_recv()
        deliver(u, h, xx, yy)

    def cell(axis, a, b):
        if axis == 0:
            return (x + a + 4) % 4, (y + b + 4) % 4
        return (x + b + 4) % 4, (y + a + 4) % 4

    def ways(u, h):
        first = (u + h) % 2
        return first, 1 - first, (1 if (u // 2 + h) % 2 == 0 else -1)

    def launch(u):
        for t in range(3):
            parts = []
            for zi in range(4):
                for cc in range(2):
                    parts.append(zbuf[order[u] * 4 + zi, cc, 18 * t : 18 * t + 18, :].astype(F32))
            at = (2 * q + c) * D + ylo * 576 + order[u] * UNIT
            wbuf[pl.ds(pl.multiple_of(at, 16), UNIT), 128 * t : 128 * t + 128] = jnp.concatenate(
                parts, axis=0
            ).astype(BF16)
        for h in range(2):
            first, second, _ = ways(u, h)
            for step in (1, -1):
                push(u, h, x, y, first, step)
            for step in (1, -1):
                push(u, h, x, y, second, step)
            deliver(u, h, x, y)

    def round_one(u):
        for h in range(2):
            first, second, f = ways(u, h)
            for a in (-f, f):
                blk = cell(first, a, 0)
                arrive(u, h, *blk)
                if a == -f:
                    push(u, h, *blk, first, f)
                for step in (1, -1):
                    push(u, h, *blk, second, step)
            for b in (-f, f):
                blk = cell(first, 0, b)
                arrive(u, h, *blk)
                if b == -f:
                    push(u, h, *blk, second, f)

    def round_two(u):
        for h in range(2):
            first, second, f = ways(u, h)
            blk = cell(first, 2, 0)
            arrive(u, h, *blk)
            for step in (1, -1):
                push(u, h, *blk, second, step)
            for a in (-f, f):
                for b in (-f, f):
                    blk = cell(first, a, b)
                    arrive(u, h, *blk)
                    if b == -f:
                        push(u, h, *blk, second, f)

    def round_three(u):
        for h in range(2):
            first, second, f = ways(u, h)
            arrive(u, h, *cell(first, 0, 2))
            for b in (-f, f):
                blk = cell(first, 2, b)
                arrive(u, h, *blk)
                if b == -f:
                    push(u, h, *blk, second, f)
            for a in (-f, f):
                arrive(u, h, *cell(first, a, 2))

    def round_four(u):
        for h in range(2):
            first, _, _ = ways(u, h)
            arrive(u, h, *cell(first, 2, 2))

    def zstep(k):
        for d in (2 * k - 1, 2 * k):
            zwait(-d)
            zwait(d)
        for step in (1, 2):
            zforward(-2 * k, step)
            zforward(2 * k, -step)
        for d in (2 * k - 1, 2 * k):
            exchange(0, d)
            exchange(0, -d)

    exchange_home(0)
    zstep(1)
    zstep(2)
    launch(0)
    zstep(3)
    round_one(0)
    zstep(4)
    launch(1)
    round_two(0)
    zstep(5)
    round_one(1)
    round_three(0)
    zstep(6)
    launch(2)
    round_two(1)
    zstep(7)
    round_one(2)
    zwait(-15)
    zwait(15)
    exchange(0, 15)
    exchange(0, -15)
    launch(3)
    exchange_home(1)
    for d in range(1, NZ):
        exchange(1, d)
        exchange(1, -d)
    round_four(0)
    round_three(1)
    round_two(2)
    round_one(3)
    round_four(1)
    round_three(2)
    round_two(3)
    round_four(2)
    round_three(3)
    round_four(3)
    half = wbuf.at[sizes(8 * D)]
    pltpu.make_async_copy(half, half, d_recv).wait()

    head_dim = D // HEADS
    factor = 1.0 / math.sqrt(head_dim)
    gain = gain_ref[...]

    def temporal(p):
        arrived = abuf.at[sizes(63)]
        pltpu.make_async_copy(arrived, arrived, a_recv.at[p]).wait()
        rows = abuf[64 * p : 64 * p + 64].astype(F32)
        xr = rows[:, 0:1, :].reshape(64, D)
        g = rows[:, 1:2, :].reshape(64, D)
        gh = g.astype(BF16)
        mean = jnp.mean(xr, axis=-1, keepdims=True)
        centred = xr - mean
        inv_std = lax.rsqrt(jnp.mean(centred * centred, axis=-1, keepdims=True) + EPS)
        normal = centred * inv_std
        normed = (normal * gain).astype(BF16)
        for j in range(9):
            qkv_s[:, CH * j : CH * j + CH] = (
                mm(normed, wbuf[j * D : j * D + D, :], NN) + bias_ref[:, CH * j : CH * j + CH]
            ).astype(BF16)
        acc = None
        for j in range(3):
            part = mm(gh[:, CH * j : CH * j + CH], wbuf[(9 + j) * D : (10 + j) * D, :], NT)
            acc = part if acc is None else acc + part
        ga_s[0:64, :] = acc.astype(BF16)
        for h in range(HEADS):
            lo, hi = h * head_dim, (h + 1) * head_dim
            qh, kh = qkv_s[:, lo:hi], qkv_s[:, D + lo : D + hi]
            gq, gk, gv = grads_of(
                softmax_of(qh, kh, factor, None), qh, kh, qkv_s[:, 2 * D + lo : 2 * D + hi],
                ga_s[0:64, lo:hi], factor,
            )
            dq_s[:, lo:hi] = gq
            dq_s[:, D + lo : D + hi] = gk
            dq_s[:, 2 * D + lo : 2 * D + hi] = gv
        acc = None
        for j in range(9):
            part = mm(dq_s[:, CH * j : CH * j + CH], wbuf[j * D : j * D + D, :], NT)
            acc = part if acc is None else acc + part
        hat = acc * gain
        branch = inv_std * (
            hat
            - jnp.mean(hat, axis=-1, keepdims=True)
            - normal * jnp.mean(hat * normal, axis=-1, keepdims=True)
        )
        low = branch[:, :WIDE].reshape(64, 1, WIDE)
        high = jnp.concatenate(
            [branch[:, WIDE:], jnp.zeros((64, 2 * WIDE - D), F32)], axis=1
        ).reshape(64, 1, WIDE)
        bsrc[64 * p : 64 * p + 64] = jnp.concatenate([low, high], axis=1).astype(BF16)
        for dz in (8, 7, 9, 6, 10, 5, 11, 4, 12, 3, 13, 2, 14, 1, 15):
            zz = (z + dz) % NZ

            def back(i, carry):
                t = ((ylo + i // 2) % 2) * 32 + zz * 2 + (c + i) % 2
                pltpu.make_async_remote_copy(
                    bsrc.at[64 * p + t], brecv.at[64 * p + s], b_send, b_recv,
                    device_id={"clip": q, "seq": t}, device_id_type=MESH,
                ).start()
                return carry

            lax.fori_loop(0, 4, back, 0)
        for yl, cc in ((1 - ylo, c), (1 - ylo, 1 - c), (ylo, 1 - c)):
            t = yl * 32 + z * 2 + cc
            pltpu.make_async_remote_copy(
                bsrc.at[64 * p + t], brecv.at[64 * p + s], b_send, b_recv,
                device_id={"clip": q, "seq": t}, device_id_type=MESH,
            ).start()
        brecv[64 * p + s] = bsrc[64 * p + s]
        sums[0:1, :] += jnp.sum(acc * normal, axis=0, keepdims=True)
        for j in range(3):
            sums[1 + j : 2 + j, :] += jnp.sum(
                dq_s[:, D * j : D * j + D].astype(F32), axis=0, keepdims=True
            )

    temporal(0)
    temporal(1)

    sums[4:5, :] = jnp.sum(g_ref[...].astype(F32), axis=0, keepdims=True)
    for h in range(HEADS):
        lo, hi = h * head_dim, (h + 1) * head_dim
        sw_s[h] = softmax_of(sq_ref[:, lo:hi], sq_ref[:, D + lo : D + hi], factor, None)

    everyone = brecv.at[sizes(126)]
    pltpu.make_async_copy(everyone, everyone, b_recv).wait()
    pieces = []
    for p in range(2):
        rows = brecv[64 * p : 64 * p + 64].astype(F32)
        pieces.append(jnp.concatenate([rows[:, 0:1, :], rows[:, 1:2, : D - WIDE]], axis=2))
    branch = jnp.concatenate(pieces, axis=1).reshape(128, D)
    resid = (g_ref[...].astype(F32) + branch).astype(BF16)
    resid_ref[...] = resid
    sums[8:9, :] = jnp.sum(resid.astype(F32), axis=0, keepdims=True)
    acc = None
    for j in range(3):
        part = mm(resid_ref[:, CH * j : CH * j + CH], wbuf[(12 + j) * D : (13 + j) * D, :], NT)
        acc = part if acc is None else acc + part
    ga_s[...] = acc.astype(BF16)
    for h in range(HEADS):
        lo, hi = h * head_dim, (h + 1) * head_dim
        gq, gk, gv = grads_of(
            sw_s[h], sq_ref[:, lo:hi], sq_ref[:, D + lo : D + hi],
            sq_ref[:, 2 * D + lo : 2 * D + hi], ga_s[:, lo:hi], factor,
        )
        dqkv_ref[:, lo:hi] = gq
        dqkv_ref[:, D + lo : D + hi] = gk
        dqkv_ref[:, 2 * D + lo : 2 * D + hi] = gv
    for j in range(3):
        sums[5 + j : 6 + j, :] = jnp.sum(
            dqkv_ref[:, D * j : D * j + D].astype(F32), axis=0, keepdims=True
        )

    pair = pltpu.make_async_remote_copy(
        sums, mate, m_send, m_recv, device_id=sib, device_id_type=MESH
    )
    pair.start()
    pair.wait_recv()
    both = sums[...] + mate[...]
    mine = jnp.where(c == 0, both[0:8], jnp.concatenate([both[5:9], both[9:13]], axis=0))
    for k in range(NZ):
        for yl in range(2):
            lo = yl * 576 + 36 * k
            slab[k, :, 36 * yl : 36 * yl + 36] = mine[:, lo : lo + 36]

    def xy_peer(i):
        return (x + i // 4) % 4, (y + i % 4) % 4

    def zsend(i, carry):
        k = (z + i) % NZ
        pltpu.make_async_remote_copy(
            slab.at[k], zin.at[z], z_send, z_recv, device_id=dev(x, y, k, c), device_id_type=MESH
        ).start()
        return carry

    def psend(i, carry):
        pltpu.make_async_remote_copy(
            zin.at[NZ], pin.at[x * 4 + y], q_send, q_recv,
            device_id=dev(*xy_peer(i), z, c), device_id_type=MESH,
        ).start()
        return carry

    lax.fori_loop(1, 16, zsend, 0)
    zin[z] = slab[z]
    pltpu.make_async_copy(zin.at[pl.ds(0, 15)], zin.at[pl.ds(0, 15)], z_recv).wait()
    zsum = jnp.sum(zin[0:NZ], axis=0)
    zin[NZ] = zsum
    lax.fori_loop(1, 16, psend, 0)
    pin[x * 4 + y] = zsum
    pltpu.make_async_copy(pin.at[pl.ds(0, 15)], pin.at[pl.ds(0, 15)], q_recv).wait()
    psum = jnp.sum(pin[...], axis=0)
    fin[c] = psum
    last = pltpu.make_async_remote_copy(
        fin.at[c], fin.at[c], f_send, f_recv, device_id=sib, device_id_type=MESH
    )
    last.start()
    pltpu.make_async_remote_copy(
        fin.at[c], fin.at[1 - c], f_send, f_recv, device_id=sib, device_id_type=MESH
    ).wait_recv()
    total = jnp.concatenate([fin[0, 0:5], fin[1, 0:4]], axis=0)
    part = ylo * 2 + c
    pick = total[:, 0:18]
    for k in range(1, 4):
        pick = jnp.where(part == k, total[:, 18 * k : 18 * k + 18], pick)
    tot_ref[...] = gsum_ref[...] + pick * (1.0 / math.sqrt(tokens))

    swap.wait_send()
    pair.wait_send()
    last.wait_send()

    def drain(ref, rows, sem):
        view = ref.at[sizes(rows)]
        pltpu.make_async_copy(view, view, sem).wait()

    drain(asrc, 126, a_send)
    drain(bsrc, 126, b_send)
    drain(zin, 15, z_send)
    drain(pin, 15, q_send)
    drain(wbuf, 60 * UNIT, p_send)
    drain(wbuf, 8 * D, d_send)
    for k in range(8):
        for step in (1, -1, 2, -2):
            back = -2 * k if step > 0 else 2 * k

            @pl.when(jnp.logical_and(on_line(back), on_line(step)))
            def _():
                zcopy(z + back, step).wait_send()


def block(ws, x, g, sq, gain, bias, gsum, tokens):
    vm = pl.BlockSpec(memory_space=pltpu.VMEM)
    dma = pltpu.SemaphoreType.DMA
    return pl.pallas_call(
        functools.partial(block_kernel, tokens),
        out_shape=(
            jax.ShapeDtypeStruct((128, D), BF16),
            jax.ShapeDtypeStruct((128, 3 * D), BF16),
            jax.ShapeDtypeStruct((9, D // 64), F32),
        ),
        in_specs=[pl.BlockSpec(memory_space=pl.ANY)] + [vm] * 6,
        out_specs=(vm, vm, vm),
        scratch_shapes=[
            pltpu.VMEM((NZ, 2, 54, 128), BF16),
            pltpu.VMEM((NCH * D, CH), BF16),
            pltpu.VMEM((128, 2, D), BF16),
            pltpu.VMEM((128, 2, D), BF16),
            pltpu.VMEM((64, 3 * D), BF16),
            pltpu.VMEM((128, D), BF16),
            pltpu.VMEM((64, 3 * D), BF16),
            pltpu.VMEM((HEADS, 128, 128), F32),
            pltpu.VMEM((128, 2, WIDE), BF16),
            pltpu.VMEM((128, 2, WIDE), BF16),
            pltpu.VMEM((16, D), F32),
            pltpu.VMEM((16, D), F32),
            pltpu.VMEM((NZ, 8, 128), F32),
            pltpu.VMEM((NZ + 1, 8, 128), F32),
            pltpu.VMEM((16, 8, 128), F32),
            pltpu.VMEM((2, 8, 128), F32),
            dma, dma, dma, dma((4 * NZ,)), dma((NZ,)), dma, dma((2,)), dma, dma((128,)), dma, dma,
            dma, dma, dma, dma, dma, dma, dma, dma, dma, dma,
        ],
        compiler_params=pltpu.CompilerParams(
            collective_id=0, has_side_effects=True, vmem_limit_bytes=56 << 20
        ),
        name="block",
    )(ws, x, g, sq, gain, bias, gsum)


def per_device(
    block_input, out_grad, spatial_qkv, norm_gain, qkv_weight, qkv_bias, out_weight,
    spatial_out_weight, grad_sums,
):
    rows = qkv_weight.shape[0]
    pad = jnp.zeros((rows, CH), BF16)
    w = jnp.concatenate([qkv_weight, out_weight, spatial_out_weight, pad], axis=1)
    ws = w.reshape(rows, NCH, 3, 128).transpose(1, 2, 0, 3).reshape(NCH, 3 * rows, 128)
    tokens = 128 * lax.axis_size("seq") * lax.axis_size("clip")
    resid, sgrad, totals = block(
        ws, block_input.reshape(128, D), out_grad.reshape(128, D), spatial_qkv.reshape(128, 3 * D),
        norm_gain.reshape(1, D), qkv_bias.reshape(1, 3 * D), grad_sums, tokens,
    )
    return resid.reshape(1, 1, 128, D), sgrad.reshape(1, 1, 128, 3 * D), totals


def solution(mesh):
    in_specs = (
        P("clip", "seq", None, None),
        P("clip", "seq", None, None),
        P("clip", "seq", None, None),
        P(),
        P("seq", None),
        P(),
        P("seq", None),
        P("seq", None),
        P(None, "seq"),
    )
    out_specs = (P("clip", "seq", None, None), P("clip", "seq", None, None), P(None, "seq"))
    return jax.shard_map(
        per_device, mesh=mesh, in_specs=in_specs, out_specs=out_specs, check_vma=False
    )
```

time: 143 us -> 154 us (1.077)
  Pallas kernels: 131 us -> 143 us
    pallas_call x2 -> x1, Pallas kernels: 131 us -> 143 us  [block(): pl.pallas_call(functools.partial(block_kernel, tokens), out_shape=(jax.Sh...]
    unnamed x11 -> x7, local copies, waits for them, and re-layouts: 5.64 us -> 4.46 us
where the time goes in v3:
time: 154 us; the launch traced here: 153 us
  Pallas kernels  143 us (93%)
  local copies, waits for them, and re-layouts  8.22 us (5%)
    pallas_call x1, Pallas kernels, block(): pl.pallas_call(functools.partial(block_kernel, tokens), out_shape=(jax.Sh...  143 us
    unnamed x7, local copies, waits for them, and re-layouts  4.46 us

profile of v3, /device:TPU:1, one launch (start us, length us, event | category | flops | bytes accessed | tf_op | source)
XLA Modules:
  0.0 153.3 jit_solution(8661522877098152037)
XLA Ops:
  0.6 0.0 copy-start
  0.6 1.3 reshape.38.gain_ref
  2.0 1.3 reshape.39.bias_ref
  3.3 0.0 copy-done
  3.3 1.0 maximum_maximum_fusion
  4.3 0.3 reshape.33
  4.7 0.7 copy.14.ws
  5.4 143.4 %block.1 = (bf16[128,1152]{1,0:T(8,128)(2,1)}, bf16[128,3456]{1,0:T(8,128)(2,1)}, f32[9,18]{1,0:T(8,128)}) custom-call(bf16[16,54,128]{2,1,0:T(8,128)(2,1)} %copy.14.ws, bf16[128,1152]{1,0:T(8,128)(2,1)} %bitcast.12, bf16[128,1152]{1,0:T(8,128)(2,1)} %bitcast.13, bf16[128,3456]{1,0:T(8,128)(2,1)} %bitcast.10, f32[1,1152]{1,0:T(1,128)} %reshape.38.gain_ref, ...), custom_call_target="tpu_custom_call" | custom-call | tf_op jit(solution)/shard_map/block/pallas_call | solution.py:526
  148.8 1.7 %copy.18 = bf16[1,1,128,1152]{3,2,1,0:T(8,128)(2,1)} copy(bf16[1,1,128,1152]{3,2,1,0:T(8,128)(2,1)} %bitcast.11) | data formatting | bytes 589824
  150.5 0.0 copy-start.1
  150.5 2.2 %copy.19 = bf16[1,1,128,3456]{3,2,1,0:T(8,128)(2,1)} copy(bf16[1,1,128,3456]{3,2,1,0:T(8,128)(2,1)} %bitcast.8) | data formatting | bytes 1769472
  152.7 0.0 copy-done.1
  152.7 0.6 copy.20
  (3 shorter events, 0.0 us)
Async XLA Ops:
  0.6 2.7 %copy-start = (bf16[18,1152]{1,0:T(8,128)(2,1)S(1)}, bf16[18,1152]{1,0:T(8,128)(2,1)}, u32[]{:S(2)}) copy-start(bf16[18,1152]{1,0:T(8,128)(2,1)} %param.16) | copy-start | bytes 124420
  150.5 2.2 %copy-start.1 = (f32[9,18]{1,0:T(8,128)S(1)}, f32[9,18]{1,0:T(8,128)}, u32[]{:S(2)}) copy-start(f32[9,18]{1,0:T(8,128)} %get-tuple-element.14) | copy-start | bytes 1948

commit v4 on v2

v4 whole, which is shorter than its diff:
```python
import functools
import math

import jax
import jax.numpy as jnp
from jax import lax
from jax.experimental import pallas as pl
from jax.experimental.pallas import tpu as pltpu
from jax.sharding import PartitionSpec as P

HEADS = 16
EPS = 1e-06
MESH = pl.DeviceIdType.MESH
F32 = jnp.float32
BF16 = jnp.bfloat16

D = 1152
CH = 384
NCH = 16
NZ = 16
UNIT = 144
HALF = ((0, 80), (80, 64))


def dev(x, y, z, c):
    return {"clip": x * 2 + y // 2, "seq": (y % 2) * 32 + z * 2 + c}


def place():
    s, q = lax.axis_index("seq"), lax.axis_index("clip")
    x = q // 2
    y = (q % 2) * 2 + s // 32
    z = (s // 2) % 16
    c = s % 2
    return x, y, z, c


NT = (((1,), (1,)), ((), ()))
TN = (((0,), (0,)), ((), ()))
NN = (((1,), (0,)), ((), ()))


def mm(a, b, dims):
    return lax.dot_general(a, b, dims, preferred_element_type=F32)


def softmax_of(qh, kh, factor, mask):
    scores = mm(qh, kh, NT) * factor
    if mask is not None:
        scores = jnp.where(mask, scores, -jnp.inf)
    top = jnp.max(scores, axis=-1, keepdims=True)
    e = jnp.exp(scores - top)
    return e / jnp.sum(e, axis=-1, keepdims=True)


def grads_of(weights, qh, kh, vh, gh, factor):
    grad_value = mm(weights.astype(BF16), gh, TN)
    grad_weight = mm(gh, vh, NT)
    r = jnp.sum(weights * grad_weight, axis=-1, keepdims=True)
    gs = (weights * (grad_weight - r) * factor).astype(BF16)
    grad_query = mm(gs, kh, NN)
    grad_key = mm(gs, qh, TN)
    return grad_query.astype(BF16), grad_key.astype(BF16), grad_value.astype(BF16)


def sizes(rows):
    return pl.ds(0, rows)


def block_kernel(
    tokens, ws, x_ref, g_ref, sq_ref, gain_ref, bias_ref, gsum_ref, resid_ref, dqkv_ref, tot_ref,
    zbuf, wbuf, asrc, abuf, qkv_s, g_s, ga_s, dq_s, sw_s, bsrc, brecv, sums, mate, slab, zin, pin, fin,
    loc, swap_s, swap_r, zg_send, zg_recv, a_send, a_recv, p_send, p_recv, d_send, d_recv,
    b_send, b_recv, m_send, m_recv, z_send, z_recv, q_send, q_recv, f_send, f_recv,
):
    x, y, z, c = place()
    s, q = lax.axis_index("seq"), lax.axis_index("clip")
    ylo = s // 32
    sib = dev(x, y, z, 1 - c)

    def near(axis, step):
        if axis == 0:
            return (x + step + 4) % 4, y
        return x, (y + step + 4) % 4

    barrier = pltpu.get_barrier_semaphore()
    partners = [
        sib,
        dev(*near(0, 1), z, c),
        dev(*near(0, -1), z, c),
        dev(*near(1, 1), z, c),
        dev(*near(1, -1), z, c),
        {"clip": q, "seq": (1 - ylo) * 32 + z * 2 + 1 - c},
        dev(x, y, (z + 1) % NZ, c),
        dev(x, y, (z + NZ - 1) % NZ, c),
        dev(x, y, (z + 2) % NZ, c),
        dev(x, y, (z + NZ - 2) % NZ, c),
    ]
    for p in partners:
        pl.semaphore_signal(barrier, inc=1, device_id=p, device_id_type=MESH)
    keep = pltpu.make_async_copy(ws.at[2 * q + c], zbuf.at[z, c], loc)
    keep.start()
    sums[...] = jnp.zeros((16, D), F32)
    slab[...] = jnp.zeros((NZ, 8, 128), F32)
    pl.semaphore_wait(barrier, len(partners))

    swap = pltpu.make_async_remote_copy(
        ws.at[2 * q + 1 - c], zbuf.at[z, c], swap_s, swap_r, device_id=sib, device_id_type=MESH
    )
    swap.start()
    keep.wait()
    pltpu.make_async_remote_copy(
        ws.at[2 * q + 1 - c], zbuf.at[z, 1 - c], swap_s, swap_r, device_id=sib, device_id_type=MESH
    ).wait_recv()

    def zcopy(origin, step):
        o = (origin + 2 * NZ) % NZ
        return pltpu.make_async_remote_copy(
            zbuf.at[o], zbuf.at[o], zg_send, zg_recv.at[o],
            device_id=dev(x, y, (z + step + NZ) % NZ, c), device_id_type=MESH,
        )

    def zwait(origin):
        zcopy(origin, 1).wait_recv()

    for step in (1, -1, 2, -2):
        zcopy(z, step).start()

    x3 = x_ref[...].astype(F32).reshape(64, 2, D)
    g3 = g_ref[...].astype(F32).reshape(64, 2, D)
    asrc[...] = jnp.concatenate([x3, g3], axis=1).astype(BF16)

    def exchange(dist):
        zz = (z + dist + NZ) % NZ

        def one(i, carry):
            t = ((ylo + i // 2) % 2) * 32 + zz * 2 + (c + i) % 2
            pltpu.make_async_remote_copy(
                asrc.at[t], abuf.at[s], a_send, a_recv,
                device_id={"clip": q, "seq": t}, device_id_type=MESH,
            ).start()
            return carry

        lax.fori_loop(0, 4, one, 0)

    def exchange_home():
        for yl, cc in ((1 - ylo, c), (1 - ylo, 1 - c), (ylo, 1 - c)):
            t = yl * 32 + z * 2 + cc
            pltpu.make_async_remote_copy(
                asrc.at[t], abuf.at[s], a_send, a_recv,
                device_id={"clip": q, "seq": t}, device_id_type=MESH,
            ).start()
        abuf[s] = asrc[s]

    group = z // 4
    order = [group, group + 1 - 2 * (group % 2), 2 - group // 2, 3 - 3 * (group // 2)]

    def spot(u, h, xx, yy):
        off, n = HALF[h]
        at = (2 * (xx * 2 + yy // 2) + c) * D + (yy % 2) * 576 + order[u] * UNIT + off
        return pl.ds(pl.multiple_of(at, 16), n)

    def push(u, h, xx, yy, axis, step):
        rows = spot(u, h, xx, yy)
        nx, ny = near(axis, step)
        pltpu.make_async_remote_copy(
            wbuf.at[rows], wbuf.at[rows], p_send, p_recv.at[(u * 2 + h) * 16 + xx * 4 + yy],
            device_id=dev(nx, ny, z, c), device_id_type=MESH,
        ).start()

    def deliver(u, h, xx, yy):
        rows = spot(u, h, xx, yy)
        pltpu.make_async_remote_copy(
            wbuf.at[rows], wbuf.at[rows], d_send, d_recv, device_id=sib, device_id_type=MESH
        ).start()

    def arrive(u, h, xx, yy):
        rows = spot(u, h, xx, yy)
        pltpu.make_async_remote_copy(
            wbuf.at[rows], wbuf.at[rows], p_send, p_recv.at[(u * 2 + h) * 16 + xx * 4 + yy],
            device_id=sib, device_id_type=MESH,
        ).wait_recv()
        deliver(u, h, xx, yy)

    def cell(axis, a, b):
        if axis == 0:
            return (x + a + 4) % 4, (y + b + 4) % 4
        return (x + b + 4) % 4, (y + a + 4) % 4

    def ways(u, h):
        first = (u + h) % 2
        return first, 1 - first, (1 if (u // 2 + h) % 2 == 0 else -1)

    def launch(u):
        for t in range(3):
            parts = []
            for zi in range(4):
                for cc in range(2):
                    parts.append(zbuf[order[u] * 4 + zi, cc, 18 * t : 18 * t + 18, :].astype(F32))
            at = (2 * q + c) * D + ylo * 576 + order[u] * UNIT
            wbuf[pl.ds(pl.multiple_of(at, 16), UNIT), 128 * t : 128 * t + 128] = jnp.concatenate(
                parts, axis=0
            ).astype(BF16)
        for h in range(2):
            first, second, _ = ways(u, h)
            for step in (1, -1):
                push(u, h, x, y, first, step)
            for step in (1, -1):
                push(u, h, x, y, second, step)
            deliver(u, h, x, y)

    def round_one(u):
        for h in range(2):
            first, second, f = ways(u, h)
            for a in (-f, f):
                blk = cell(first, a, 0)
                arrive(u, h, *blk)
                if a == -f:
                    push(u, h, *blk, first, f)
                for step in (1, -1):
                    push(u, h, *blk, second, step)
            for b in (-f, f):
                blk = cell(first, 0, b)
                arrive(u, h, *blk)
                if b == -f:
                    push(u, h, *blk, second, f)

    def round_two(u):
        for h in range(2):
            first, second, f = ways(u, h)
            blk = cell(first, 2, 0)
            arrive(u, h, *blk)
            for step in (1, -1):
                push(u, h, *blk, second, step)
            for a in (-f, f):
                for b in (-f, f):
                    blk = cell(first, a, b)
                    arrive(u, h, *blk)
                    if b == -f:
                        push(u, h, *blk, second, f)

    def round_three(u):
        for h in range(2):
            first, second, f = ways(u, h)
            arrive(u, h, *cell(first, 0, 2))
            for b in (-f, f):
                blk = cell(first, 2, b)
                arrive(u, h, *blk)
                if b == -f:
                    push(u, h, *blk, second, f)
            for a in (-f, f):
                arrive(u, h, *cell(first, a, 2))

    def round_four(u):
        for h in range(2):
            first, _, _ = ways(u, h)
            arrive(u, h, *cell(first, 2, 2))

    for k in (1, 2, 3):
        for d in (2 * k - 1, 2 * k):
            zwait(z - d)
            zwait(z + d)
        zcopy(z - 2 * k, 1).start()
        zcopy(z + 2 * k, -1).start()
        zcopy(z - 2 * k, 2).start()
        if k < 3:
            zcopy(z + 2 * k, -2).start()
        if k == 1:
            exchange_home()
        for d in (2 * k - 1, 2 * k):
            exchange(d)
            exchange(-d)
        if k == 2:
            launch(0)
        if k == 3:
            round_one(0)
    zwait(z - 7)
    zwait(z + 7)
    zwait(z - 8)
    exchange(7)
    exchange(-7)
    exchange(8)
    launch(1)
    launch(2)
    round_two(0)
    launch(3)
    round_one(1)
    round_one(2)
    round_three(0)
    round_one(3)
    round_two(1)
    round_two(2)
    round_four(0)
    round_two(3)
    round_three(1)
    round_three(2)
    round_three(3)
    round_four(1)
    round_four(2)
    round_four(3)

    head_dim = D // HEADS
    factor = 1.0 / math.sqrt(head_dim)
    arrived = abuf.at[sizes(63)]
    pltpu.make_async_copy(arrived, arrived, a_recv).wait()
    rows = abuf[...].astype(F32)
    xr = rows[:, 0:2, :].reshape(128, D)
    g = rows[:, 2:4, :].reshape(128, D)
    sums[4:5, :] = jnp.sum(g, axis=0, keepdims=True)
    g_s[...] = g.astype(BF16)
    mean = jnp.mean(xr, axis=-1, keepdims=True)
    centred = xr - mean
    inv_std = lax.rsqrt(jnp.mean(centred * centred, axis=-1, keepdims=True) + EPS)
    normal = centred * inv_std
    gain = gain_ref[...].reshape(1, D)
    normed = (normal * gain).astype(BF16)
    half = wbuf.at[sizes(8 * D)]
    pltpu.make_async_copy(half, half, d_recv).wait()
    for j in range(9):
        qkv_s[:, CH * j : CH * j + CH] = (
            mm(normed, wbuf[j * D : j * D + D, :], NN) + bias_ref[CH * j : CH * j + CH].reshape(1, CH)
        ).astype(BF16)
    acc = None
    for j in range(3):
        part = mm(g_s[:, CH * j : CH * j + CH], wbuf[(9 + j) * D : (10 + j) * D, :], NT)
        acc = part if acc is None else acc + part
    ga_s[...] = acc.astype(BF16)
    ri = lax.broadcasted_iota(jnp.int32, (128, 128), 0)
    ci = lax.broadcasted_iota(jnp.int32, (128, 128), 1)
    mask = (ri & 1) == (ci & 1)
    for h in range(HEADS):
        lo, hi = h * head_dim, (h + 1) * head_dim
        qh, kh = qkv_s[:, lo:hi], qkv_s[:, D + lo : D + hi]
        gq, gk, gv = grads_of(
            softmax_of(qh, kh, factor, mask), qh, kh, qkv_s[:, 2 * D + lo : 2 * D + hi],
            ga_s[:, lo:hi], factor,
        )
        dq_s[:, lo:hi] = gq
        dq_s[:, D + lo : D + hi] = gk
        dq_s[:, 2 * D + lo : 2 * D + hi] = gv
    acc = None
    for j in range(9):
        part = mm(dq_s[:, CH * j : CH * j + CH], wbuf[j * D : j * D + D, :], NT)
        acc = part if acc is None else acc + part
    grad_normed = acc
    hat = grad_normed * gain
    branch = inv_std * (
        hat
        - jnp.mean(hat, axis=-1, keepdims=True)
        - normal * jnp.mean(hat * normal, axis=-1, keepdims=True)
    )
    bsrc[...] = branch.reshape(64, 2, D).astype(BF16)

    for dz in (8, 7, 9, 6, 10, 5, 11, 4, 12, 3, 13, 2, 14, 1, 15):
        zz = (z + dz) % NZ

        def back(i, carry):
            t = ((ylo + i // 2) % 2) * 32 + zz * 2 + (c + i) % 2
            pltpu.make_async_remote_copy(
                bsrc.at[t], brecv.at[s], b_send, b_recv,
                device_id={"clip": q, "seq": t}, device_id_type=MESH,
            ).start()
            return carry

        lax.fori_loop(0, 4, back, 0)
    for yl, cc in ((1 - ylo, c), (1 - ylo, 1 - c), (ylo, 1 - c)):
        t = yl * 32 + z * 2 + cc
        pltpu.make_async_remote_copy(
            bsrc.at[t], brecv.at[s], b_send, b_recv,
            device_id={"clip": q, "seq": t}, device_id_type=MESH,
        ).start()
    brecv[s] = bsrc[s]

    sums[0:1, :] = jnp.sum(grad_normed * normal, axis=0, keepdims=True)
    for j in range(3):
        sums[1 + j : 2 + j, :] = jnp.sum(
            dq_s[:, D * j : D * j + D].astype(F32), axis=0, keepdims=True
        )
    for h in range(HEADS):
        lo, hi = h * head_dim, (h + 1) * head_dim
        sw_s[h] = softmax_of(sq_ref[:, lo:hi], sq_ref[:, D + lo : D + hi], factor, None)

    pltpu.make_async_copy(brecv.at[pl.ds(0, 63)], brecv.at[pl.ds(0, 63)], b_recv).wait()
    resid = (g_ref[...].astype(F32) + brecv[...].astype(F32).reshape(128, D)).astype(BF16)
    resid_ref[...] = resid
    sums[8:9, :] = jnp.sum(resid.astype(F32), axis=0, keepdims=True)
    acc = None
    for j in range(3):
        part = mm(resid_ref[:, CH * j : CH * j + CH], wbuf[(12 + j) * D : (13 + j) * D, :], NT)
        acc = part if acc is None else acc + part
    ga_s[...] = acc.astype(BF16)
    for h in range(HEADS):
        lo, hi = h * head_dim, (h + 1) * head_dim
        gq, gk, gv = grads_of(
            sw_s[h], sq_ref[:, lo:hi], sq_ref[:, D + lo : D + hi],
            sq_ref[:, 2 * D + lo : 2 * D + hi], ga_s[:, lo:hi], factor,
        )
        dqkv_ref[:, lo:hi] = gq
        dqkv_ref[:, D + lo : D + hi] = gk
        dqkv_ref[:, 2 * D + lo : 2 * D + hi] = gv
    for j in range(3):
        sums[5 + j : 6 + j, :] = jnp.sum(
            dqkv_ref[:, D * j : D * j + D].astype(F32), axis=0, keepdims=True
        )

    pair = pltpu.make_async_remote_copy(
        sums, mate, m_send, m_recv, device_id=sib, device_id_type=MESH
    )
    pair.start()
    pair.wait_recv()
    both = sums[...] + mate[...]
    mine = jnp.where(c == 0, both[0:8], jnp.concatenate([both[5:9], both[9:13]], axis=0))
    for k in range(NZ):
        for yl in range(2):
            lo = yl * 576 + 36 * k
            slab[k, :, 36 * yl : 36 * yl + 36] = mine[:, lo : lo + 36]

    def xy_peer(i):
        return (x + i // 4) % 4, (y + i % 4) % 4

    def zsend(i, carry):
        k = (z + i) % NZ
        pltpu.make_async_remote_copy(
            slab.at[k], zin.at[z], z_send, z_recv, device_id=dev(x, y, k, c), device_id_type=MESH
        ).start()
        return carry

    def psend(i, carry):
        pltpu.make_async_remote_copy(
            zin.at[NZ], pin.at[x * 4 + y], q_send, q_recv,
            device_id=dev(*xy_peer(i), z, c), device_id_type=MESH,
        ).start()
        return carry

    lax.fori_loop(1, 16, zsend, 0)
    zin[z] = slab[z]
    pltpu.make_async_copy(zin.at[pl.ds(0, 15)], zin.at[pl.ds(0, 15)], z_recv).wait()
    zsum = jnp.sum(zin[0:NZ], axis=0)
    zin[NZ] = zsum
    lax.fori_loop(1, 16, psend, 0)
    pin[x * 4 + y] = zsum
    pltpu.make_async_copy(pin.at[pl.ds(0, 15)], pin.at[pl.ds(0, 15)], q_recv).wait()
    psum = jnp.sum(pin[...], axis=0)
    fin[c] = psum
    last = pltpu.make_async_remote_copy(
        fin.at[c], fin.at[c], f_send, f_recv, device_id=sib, device_id_type=MESH
    )
    last.start()
    pltpu.make_async_remote_copy(
        fin.at[c], fin.at[1 - c], f_send, f_recv, device_id=sib, device_id_type=MESH
    ).wait_recv()
    total = jnp.concatenate([fin[0, 0:5], fin[1, 0:4]], axis=0)
    part = ylo * 2 + c
    pick = total[:, 0:18]
    for k in range(1, 4):
        pick = jnp.where(part == k, total[:, 18 * k : 18 * k + 18], pick)
    tot_ref[...] = gsum_ref[...] + pick * (1.0 / math.sqrt(tokens))

    swap.wait_send()
    pair.wait_send()
    last.wait_send()

    def drain(ref, rows, sem):
        view = ref.at[sizes(rows)]
        pltpu.make_async_copy(view, view, sem).wait()

    drain(asrc, 63, a_send)
    drain(bsrc, 63, b_send)
    drain(zin, 15, z_send)
    drain(pin, 15, q_send)
    drain(wbuf, 60 * UNIT, p_send)
    drain(wbuf, 8 * D, d_send)
    drain(zbuf, 15, zg_send)


def block(ws, x, g, sq, gain, bias, gsum, tokens):
    vm = pl.BlockSpec(memory_space=pltpu.VMEM)
    dma = pltpu.SemaphoreType.DMA
    return pl.pallas_call(
        functools.partial(block_kernel, tokens),
        out_shape=(
            jax.ShapeDtypeStruct((128, D), BF16),
            jax.ShapeDtypeStruct((128, 3 * D), BF16),
            jax.ShapeDtypeStruct((9, D // 64), F32),
        ),
        in_specs=[pl.BlockSpec(memory_space=pl.ANY)] + [vm] * 6,
        out_specs=(vm, vm, vm),
        scratch_shapes=[
            pltpu.VMEM((NZ, 2, 54, 128), BF16),
            pltpu.VMEM((NCH * D, CH), BF16),
            pltpu.VMEM((64, 4, D), BF16),
            pltpu.VMEM((64, 4, D), BF16),
            pltpu.VMEM((128, 3 * D), BF16),
            pltpu.VMEM((128, D), BF16),
            pltpu.VMEM((128, D), BF16),
            pltpu.VMEM((128, 3 * D), BF16),
            pltpu.VMEM((HEADS, 128, 128), F32),
            pltpu.VMEM((64, 2, D), BF16),
            pltpu.VMEM((64, 2, D), BF16),
            pltpu.VMEM((16, D), F32),
            pltpu.VMEM((16, D), F32),
            pltpu.VMEM((NZ, 8, 128), F32),
            pltpu.VMEM((NZ + 1, 8, 128), F32),
            pltpu.VMEM((16, 8, 128), F32),
            pltpu.VMEM((2, 8, 128), F32),
            dma, dma, dma, dma, dma((NZ,)), dma, dma, dma, dma((128,)), dma, dma,
            dma, dma, dma, dma, dma, dma, dma, dma, dma, dma,
        ],
        compiler_params=pltpu.CompilerParams(
            collective_id=0, has_side_effects=True, vmem_limit_bytes=56 << 20
        ),
        name="block",
    )(ws, x, g, sq, gain, bias, gsum)


def per_device(
    block_input, out_grad, spatial_qkv, norm_gain, qkv_weight, qkv_bias, out_weight,
    spatial_out_weight, grad_sums,
):
    rows = qkv_weight.shape[0]
    pad = jnp.zeros((rows, CH), BF16)
    w = jnp.concatenate([qkv_weight, out_weight, spatial_out_weight, pad], axis=1)
    ws = w.reshape(rows, NCH, 3, 128).transpose(1, 2, 0, 3).reshape(NCH, 3 * rows, 128)
    tokens = 128 * lax.axis_size("seq") * lax.axis_size("clip")
    resid, sgrad, totals = block(
        ws, block_input.reshape(128, D), out_grad.reshape(128, D), spatial_qkv.reshape(128, 3 * D),
        norm_gain, qkv_bias, grad_sums, tokens,
    )
    return resid.reshape(1, 1, 128, D), sgrad.reshape(1, 1, 128, 3 * D), totals


def solution(mesh):
    in_specs = (
        P("clip", "seq", None, None),
        P("clip", "seq", None, None),
        P("clip", "seq", None, None),
        P(),
        P("seq", None),
        P(),
        P("seq", None),
        P("seq", None),
        P(None, "seq"),
    )
    out_specs = (P("clip", "seq", None, None), P("clip", "seq", None, None), P(None, "seq"))
    return jax.shard_map(
        per_device, mesh=mesh, in_specs=in_specs, out_specs=out_specs, check_vma=False
    )
```

time: 143 us -> 134 us (0.937)
  Pallas kernels: 131 us -> 127 us
  local copies, waits for them, and re-layouts: 8.96 us -> 5.57 us
    pallas_call x2 -> x1, Pallas kernels: 131 us -> 127 us  [block(): pl.pallas_call(functools.partial(block_kernel, tokens), out_shape=(jax.Sh...]
    reshape x6 -> x2, local copies, waits for them, and re-layouts: 3.28 us -> 1.08 us  [per_device(): w.reshape(rows, NCH, 3, 128).transpose(1, 2, 0, 3)]
    unnamed x11 -> x5, local copies, waits for them, and re-layouts: 5.64 us -> 4.45 us
where the time goes in v4:
time: 134 us
  Pallas kernels  127 us (95%)
  local copies, waits for them, and re-layouts  5.57 us (4%)
    pallas_call x1, Pallas kernels, block(): pl.pallas_call(functools.partial(block_kernel, tokens), out_shape=(jax.Sh...  127 us
    unnamed x5, local copies, waits for them, and re-layouts  4.45 us

profile of v4, /device:TPU:1, one launch (start us, length us, event | category | flops | bytes accessed | tf_op | source)
XLA Modules:
  0.0 134.0 jit_solution(14064771084654416703)
XLA Ops:
  0.7 1.0 maximum_maximum_fusion
  1.7 0.3 reshape.27
  2.1 0.7 copy.14.ws
  2.8 126.7 %block.1 = (bf16[128,1152]{1,0:T(8,128)(2,1)}, bf16[128,3456]{1,0:T(8,128)(2,1)}, f32[9,18]{1,0:T(8,128)}) custom-call(bf16[16,54,128]{2,1,0:T(8,128)(2,1)} %copy.14.ws, bf16[128,1152]{1,0:T(8,128)(2,1)} %bitcast.12, bf16[128,1152]{1,0:T(8,128)(2,1)} %bitcast.13, bf16[128,3456]{1,0:T(8,128)(2,1)} %bitcast.10, f32[1152]{0:T(1024)} %gain_ref.1, ...), custom_call_target="tpu_custom_call" | custom-call | tf_op jit(solution)/shard_map/block/pallas_call | solution.py:479
  129.6 1.7 %copy.18 = bf16[1,1,128,1152]{3,2,1,0:T(8,128)(2,1)} copy(bf16[1,1,128,1152]{3,2,1,0:T(8,128)(2,1)} %bitcast.11) | data formatting | bytes 589824
  131.3 0.0 copy-start
  131.3 2.2 %copy.19 = bf16[1,1,128,3456]{3,2,1,0:T(8,128)(2,1)} copy(bf16[1,1,128,3456]{3,2,1,0:T(8,128)(2,1)} %bitcast.8) | data formatting | bytes 1769472
  133.4 0.0 copy-done
  133.4 0.6 copy.20
  (3 shorter events, 0.0 us)
Async XLA Ops:
  131.3 2.2 %copy-start = (f32[9,18]{1,0:T(8,128)S(1)}, f32[9,18]{1,0:T(8,128)}, u32[]{:S(2)}) copy-start(f32[9,18]{1,0:T(8,128)} %get-tuple-element.14) | copy-start | bytes 1948

commit v5 on v4

--- a/solution.py
+++ b/solution.py
@@ -68,7 +68,7 @@
 
 
 def block_kernel(
-    tokens, ws, x_ref, g_ref, sq_ref, gain_ref, bias_ref, gsum_ref, resid_ref, dqkv_ref, tot_ref,
+    tokens, ws, x_ref, g_ref, sq_ref, gain_ref, bias_ref, resid_ref, dqkv_ref, tot_ref,
     zbuf, wbuf, asrc, abuf, qkv_s, g_s, ga_s, dq_s, sw_s, bsrc, brecv, sums, mate, slab, zin, pin, fin,
     loc, swap_s, swap_r, zg_send, zg_recv, a_send, a_recv, p_send, p_recv, d_send, d_recv,
     b_send, b_recv, m_send, m_recv, z_send, z_recv, q_send, q_recv, f_send, f_recv,
@@ -296,8 +296,6 @@
     round_three(2)
     round_three(3)
     round_four(1)
-    round_four(2)
-    round_four(3)
 
     head_dim = D // HEADS
     factor = 1.0 / math.sqrt(head_dim)
@@ -314,6 +312,9 @@
     normal = centred * inv_std
     gain = gain_ref[...].reshape(1, D)
     normed = (normal * gain).astype(BF16)
+
+    round_four(2)
+    round_four(3)
     half = wbuf.at[sizes(8 * D)]
     pltpu.make_async_copy(half, half, d_recv).wait()
     for j in range(9):
@@ -454,7 +455,7 @@
     pick = total[:, 0:18]
     for k in range(1, 4):
         pick = jnp.where(part == k, total[:, 18 * k : 18 * k + 18], pick)
-    tot_ref[...] = gsum_ref[...] + pick * (1.0 / math.sqrt(tokens))
+    tot_ref[...] = pick * (1.0 / math.sqrt(tokens))
 
     swap.wait_send()
     pair.wait_send()
@@ -473,7 +474,7 @@
     drain(zbuf, 15, zg_send)
 
 
-def block(ws, x, g, sq, gain, bias, gsum, tokens):
+def block(ws, x, g, sq, gain, bias, tokens):
     vm = pl.BlockSpec(memory_space=pltpu.VMEM)
     dma = pltpu.SemaphoreType.DMA
     return pl.pallas_call(
@@ -483,7 +484,7 @@
             jax.ShapeDtypeStruct((128, 3 * D), BF16),
             jax.ShapeDtypeStruct((9, D // 64), F32),
         ),
-        in_specs=[pl.BlockSpec(memory_space=pl.ANY)] + [vm] * 6,
+        in_specs=[pl.BlockSpec(memory_space=pl.ANY)] + [vm] * 5,
         out_specs=(vm, vm, vm),
         scratch_shapes=[
             pltpu.VMEM((NZ, 2, 54, 128), BF16),
@@ -510,7 +511,28 @@
             collective_id=0, has_side_effects=True, vmem_limit_bytes=56 << 20
         ),
         name="block",
-    )(ws, x, g, sq, gain, bias, gsum)
+    )(ws, x, g, sq, gain, bias)
+
+
+def hand_kernel(resid_ref, dqkv_ref, tot_ref, gsum_ref, resid_out, dqkv_out, tot_out):
+    resid_out[...] = resid_ref[...]
+    dqkv_out[...] = dqkv_ref[...]
+    tot_out[...] = gsum_ref[...] + tot_ref[...]
+
+
+def hand_over(resid, dqkv, tot, gsum):
+    vm = pl.BlockSpec(memory_space=pltpu.VMEM)
+    return pl.pallas_call(
+        hand_kernel,
+        out_shape=(
+            jax.ShapeDtypeStruct(resid.shape, BF16),
+            jax.ShapeDtypeStruct(dqkv.shape, BF16),
+            jax.ShapeDtypeStruct(tot.shape, F32),
+        ),
+        in_specs=[vm] * 4,
+        out_specs=(vm, vm, vm),
+        name="hand_over",
+    )(resid, dqkv, tot, gsum)
 
 
 def per_device(
@@ -524,8 +546,9 @@
     tokens = 128 * lax.axis_size("seq") * lax.axis_size("clip")
     resid, sgrad, totals = block(
         ws, block_input.reshape(128, D), out_grad.reshape(128, D), spatial_qkv.reshape(128, 3 * D),
-        norm_gain, qkv_bias, grad_sums, tokens,
-    )
+        norm_gain, qkv_bias, tokens,
+    )
+    resid, sgrad, totals = hand_over(resid, sgrad, totals, grad_sums)
     return resid.reshape(1, 1, 128, D), sgrad.reshape(1, 1, 128, 3 * D), totals
 
 

time: 134 us -> 131 us (0.978)
  local copies, waits for them, and re-layouts: 5.57 us -> 1.12 us
    unnamed x5 -> x0, local copies, waits for them, and re-layouts: 4.45 us -> none
    pallas_call x0 -> x1, Pallas kernels: none -> 2.3 us  [hand_over(): pl.pallas_call(hand_kernel, out_shape=(jax.ShapeDtypeStruct(resid.shape,...]
where the time goes in v5:
time: 131 us
  Pallas kernels  128 us (98%)
    pallas_call x1, Pallas kernels, block(): pl.pallas_call(functools.partial(block_kernel, tokens), out_shape=(jax.Sh...  126 us

profile of v5, /device:TPU:1, one launch (start us, length us, event | category | flops | bytes accessed | tf_op | source)
XLA Modules:
  0.0 131.0 jit_solution(2773550790885552942)
XLA Ops:
  0.7 1.0 maximum_maximum_fusion
  1.7 0.3 reshape.27
  2.1 0.7 copy.14.ws
  2.8 125.8 %block.1 = (bf16[128,1152]{1,0:T(8,128)(2,1)}, bf16[128,3456]{1,0:T(8,128)(2,1)}, f32[9,18]{1,0:T(8,128)}) custom-call(bf16[16,54,128]{2,1,0:T(8,128)(2,1)} %copy.14.ws, bf16[128,1152]{1,0:T(8,128)(2,1)} %bitcast.10, bf16[128,1152]{1,0:T(8,128)(2,1)} %bitcast.11, bf16[128,3456]{1,0:T(8,128)(2,1)} %bitcast.9, f32[1152]{0:T(1024)} %gain_ref.1, f32[3456]{0:T(1024)} %bias_ref.1), custom_call_target="tpu_custom_call" | custom-call | tf_op jit(solution)/shard_map/block/pallas_call | solution.py:480
  128.7 2.3 %hand_over.1 = (bf16[128,1152]{1,0:T(8,128)(2,1)}, bf16[128,3456]{1,0:T(8,128)(2,1)}, f32[9,18]{1,0:T(8,128)}) custom-call(bf16[128,1152]{1,0:T(8,128)(2,1)} %get-tuple-element.9.resid_ref, bf16[128,3456]{1,0:T(8,128)(2,1)} %get-tuple-element.10.dqkv_ref, f32[9,18]{1,0:T(8,128)} %get-tuple-element.11.tot_ref, f32[9,18]{1,0:T(8,128)} %gsum_ref.1), custom_call_target="tpu_custom_call" | custom-call | tf_op jit(solution)/shard_map/hand_over/pallas_call | solution.py:525
  (3 shorter events, 0.0 us)
